TPU v7x, 32 devices: a whole 2x2x4 slice. The times are simulated.
32 devices in a mesh: leaf: 8 (over z, y), grid: 4 (over x, core).
Axes of the slice: x: 2, y: 2, z: 4, core: 2. Of those that a mesh axis runs over, the one named last changes fastest.
Arguments:
- source_leaf: float32 [8, 4096], P(None, ('leaf', 'grid')), may hold values from -6 to 6
- block_leaf: float32 [4096, 128], P(('leaf', 'grid')), may hold values from -0.5 to 0.5
- expand_leaf: float32 [4096, 128], P(('leaf', 'grid')), may hold values from -0.5 to 0.5
- basis_leaf: float32 [4096, 256], P(('leaf', 'grid')), may hold values from -0.25 to 0.25
- pivot_leaf: float32 [4096], P(('leaf', 'grid')), may hold values from -2 to 2
- couple_leaf: float32 [8192, 128], P(('leaf', 'grid')), may hold values from -0.5 to 0.5
- ranks_leaf: int32 [8, 2], replicated, may hold values from 32 to 128
- targets_leaf: int32 [8192], P(('leaf', 'grid')), may hold values from 0 to 2047, as said below
- source_middle: float32 [8, 4096], P(None, ('leaf', 'grid')), may hold values from -6 to 6
- block_middle: float32 [4096, 128], P(('leaf', 'grid')), may hold values from -0.5 to 0.5
- expand_middle: float32 [4096, 128], P(('leaf', 'grid')), may hold values from -0.5 to 0.5
- basis_middle: float32 [4096, 256], P(('leaf', 'grid')), may hold values from -0.1875 to 0.1875
- pivot_middle: float32 [4096], P(('leaf', 'grid')), may hold values from -2 to 2
- couple_middle: float32 [4096, 128], P(('leaf', 'grid')), may hold values from -0.5 to 0.5
- ranks_middle: int32 [4, 2], replicated, may hold values from 32 to 128
- targets_middle: int32 [4096], P(('leaf', 'grid')), may hold values from 0 to 4095, as said below
- source_upper: float32 [8, 4096], P(None, ('leaf', 'grid')), may hold values from -6 to 6
- block_upper: float32 [4096, 128], P(('leaf', 'grid')), may hold values from -0.5 to 0.5
- expand_upper: float32 [4096, 128], P(('leaf', 'grid')), may hold values from -0.5 to 0.5
- basis_upper: float32 [4096, 256], P(('leaf', 'grid')), may hold values from -0.125 to 0.125
- pivot_upper: float32 [4096], P(('leaf', 'grid')), may hold values from -2 to 2
- couple_upper: float32 [4096, 128], P(('leaf', 'grid')), may hold values from -0.5 to 0.5
- ranks_upper: int32 [2, 2], replicated, may hold values from 32 to 128
- targets_upper: int32 [4096], P(('leaf', 'grid')), may hold values from 0 to 4095, as said below
- source_root: float32 [8, 4096], P(None, ('leaf', 'grid')), may hold values from -6 to 6
- block_root: float32 [4096, 128], P(('leaf', 'grid')), may hold values from -0.5 to 0.5
- expand_root: float32 [4096, 128], P(('leaf', 'grid')), may hold values from -0.5 to 0.5
- basis_root: float32 [4096, 256], P(('leaf', 'grid')), may hold values from -0.09375 to 0.09375
- pivot_root: float32 [4096], P(('leaf', 'grid')), may hold values from -2 to 2
- ranks_root: int32 [1, 2], replicated, may hold values from 32 to 128
Outputs:
- answer_leaf: float32 [8, 4096], P(None, ('leaf', 'grid'))
- answer_middle: float32 [8, 4096], P(None, ('leaf', 'grid'))
- answer_upper: float32 [8, 4096], P(None, ('leaf', 'grid'))
- answer_root: float32 [8, 4096], P(None, ('leaf', 'grid'))
Inputs may be any that keep to these rules, and one draw needn't show every extreme that they name: `targets_leaf`: within one leaf front the 1024 entries are distinct; each names a row of the parent front's row vector of 2048 rows. Split that vector's separator part and its update part each evenly, in order, over the parent's devices (leaf then grid); then the rows of one device name at most 32 rows held by any one of them, and exactly that many for some. `targets_middle`: within one middle front the entries are distinct; each names a row of the parent front's row vector of 4096 rows. Split likewise over the parent's devices, the rows of one device name at most 8 rows held by any one of them, and exactly that many for some. `targets_upper`: within one upper front the entries are distinct; each names a row of the root separator. Split evenly in order over all devices, the rows of one device name at most 4 rows held by any one of them, and exactly that many for some.
All inputs are finite; a program needn't handle non-finite values.
Results may differ from a plain program's by a relative error of at most 0.0003.
Values sent between devices are 32-bit elements; how exact they have to be, the bound alone decides.
A program may use at most 128 MiB of HBM per device.

v0:
```python
import jax
import jax.numpy as jnp
from jax import lax
from jax.sharding import PartitionSpec as P

BLOCK = 128
RANK = 128


HIGH_PRECISION = lax.Precision.HIGHEST


def from_partner(value, axis, distance):
    mask = 2**distance
    pairs = [(source, source ^ mask) for source in range(lax.axis_size(axis))]
    return lax.ppermute(value, axis, pairs)


def mult(left, right):
    return jnp.dot(left, right, precision=HIGH_PRECISION, preferred_element_type=jnp.float32)


def inner(left, right):
    return lax.dot_general(
        left,
        right,
        (((0,), (0,)), ((), ())),
        precision=HIGH_PRECISION,
        preferred_element_type=jnp.float32,
    )


def outer(left, right):
    return lax.dot_general(
        left,
        right,
        (((1,), (1,)), ((), ())),
        precision=HIGH_PRECISION,
        preferred_element_type=jnp.float32,
    )


def paired_total(partial_value, bits):
    summed = lax.psum(partial_value, "grid")
    for bit in range(bits):
        summed = summed + from_partner(summed, "leaf", bit)
    return summed


def group_total(partial_value, bits):
    return paired_total(partial_value, bits)


def upper_bit(place, bit):
    return place // (1 << bit) % 2 == 1


def group_extend(stack, bits, place):
    for bit in reversed(range(bits)):
        half = stack.shape[2] // 2
        lower_part = stack[:, :, :half]
        upper_part = stack[:, :, half:]
        flag = upper_bit(place, bit)
        keep = jnp.where(flag, upper_part, lower_part)
        send = jnp.where(flag, lower_part, upper_part)
        stack = keep + from_partner(send, "leaf", bit)
    return lax.psum_scatter(stack, "grid", scatter_dimension=2, tiled=True)


def group_fetch(stack, bits, place):
    current = lax.all_gather(stack, "grid", axis=2, tiled=True)
    for bit in range(bits):
        other = from_partner(current, "leaf", bit)
        flag = upper_bit(place, bit)
        current = jnp.where(
            flag,
            jnp.concatenate([other, current], axis=2),
            jnp.concatenate([current, other], axis=2),
        )
    return current


def forward_level(source, incoming, block, expand, basis, pivot, ranks, bits, front):
    level_batch_index = source if incoming is None else source + incoming
    count, width = level_batch_index.shape
    tiles = block.reshape(width // BLOCK, BLOCK, BLOCK)
    local_portion = jnp.einsum(
        "anh,nhk->ank",
        level_batch_index.reshape(count, width // BLOCK, BLOCK),
        tiles,
        precision=HIGH_PRECISION,
    ).reshape(count, width)
    query_lookup = basis[:, :RANK]
    coupling_right_factor = basis[:, RANK:]
    rank_pair = lax.dynamic_index_in_dim(ranks, front, 0, keepdims=False)
    columns = jnp.arange(RANK, dtype=jnp.int32)
    head_mask_grid = (columns < rank_pair[0]).astype(jnp.float32)
    column_mask_grid = (columns < rank_pair[1]).astype(jnp.float32)
    partial_value = jnp.concatenate(
        [
            mult(level_batch_index, query_lookup),
            mult(local_portion, coupling_right_factor),
            inner(expand, coupling_right_factor),
        ],
        axis=0,
    )
    total = group_total(partial_value, bits)
    hidden_q = total[:count] * head_mask_grid
    cross = total[2 * count :]
    intermediate_entries = local_portion + outer(hidden_q, expand)
    weight_entries = (total[count : 2 * count] + mult(hidden_q, cross)) * column_mask_grid
    return (
        intermediate_entries * pivot[None, :],
        weight_entries,
        (tiles, query_lookup, coupling_right_factor, cross, head_mask_grid, column_mask_grid),
    )


def backward_level(correction_entries, x_upd, couple, expand, parts, bits):
    tiles, query_lookup, coupling_right_factor, cross, head_mask_grid, column_mask_grid = parts
    count, width = correction_entries.shape
    if x_upd is None:
        total = group_total(mult(correction_entries, expand), bits)
        remainder_rows = correction_entries
        right_projection = total * head_mask_grid
    else:
        total = group_total(
            jnp.concatenate([mult(x_upd, couple), mult(correction_entries, expand)], axis=0), bits
        )
        solve_direction = total[:count] * column_mask_grid
        remainder_rows = correction_entries - outer(solve_direction, coupling_right_factor)
        right_projection = (total[count:] - outer(solve_direction, cross)) * head_mask_grid
    local_portion = jnp.einsum(
        "anh,nkh->ank",
        remainder_rows.reshape(count, width // BLOCK, BLOCK),
        tiles,
        precision=HIGH_PRECISION,
    ).reshape(count, width)
    return local_portion + outer(right_projection, query_lookup)


def extend(update, targets, sep_total, has_update, bits, place):
    count = update.shape[0]
    pieces = 2 if has_update else 1
    rows = sep_total * pieces
    buffer = jnp.zeros((count, rows), jnp.float32).at[:, targets].add(update)
    if has_update:
        stack = jnp.stack([buffer[:, :sep_total], buffer[:, sep_total:]])
    else:
        stack = buffer[None]
    return group_extend(stack, bits, place)


def fetch(stack, targets, bits, place):
    front_full = group_fetch(stack, bits, place)
    rows = front_full.transpose(1, 0, 2).reshape(front_full.shape[1], -1)
    return jnp.take(rows, targets, axis=1)


def shards(
    source_leaf,
    block_leaf,
    expand_leaf,
    basis_leaf,
    pivot_leaf,
    couple_leaf,
    ranks_leaf,
    targets_leaf,
    source_middle,
    block_middle,
    expand_middle,
    basis_middle,
    pivot_middle,
    couple_middle,
    ranks_middle,
    targets_middle,
    source_upper,
    block_upper,
    expand_upper,
    basis_upper,
    pivot_upper,
    couple_upper,
    ranks_upper,
    targets_upper,
    source_root,
    block_root,
    expand_root,
    basis_root,
    pivot_root,
    ranks_root,
):
    levels = [
        (
            source_leaf,
            block_leaf,
            expand_leaf,
            basis_leaf,
            pivot_leaf,
            couple_leaf,
            ranks_leaf,
            targets_leaf,
        ),
        (
            source_middle,
            block_middle,
            expand_middle,
            basis_middle,
            pivot_middle,
            couple_middle,
            ranks_middle,
            targets_middle,
        ),
        (
            source_upper,
            block_upper,
            expand_upper,
            basis_upper,
            pivot_upper,
            couple_upper,
            ranks_upper,
            targets_upper,
        ),
        (source_root, block_root, expand_root, basis_root, pivot_root, None, ranks_root, None),
    ]
    leaves = lax.axis_size("leaf")
    across = lax.axis_size("grid")
    place = lax.axis_index("leaf")
    depth = leaves.bit_length() - 1
    groups = [1, leaves // 4, leaves // 2, leaves]
    bit_counts = [0, depth - 2, depth - 1, depth]
    owners = [place // groups[level] for level in range(4)]
    inc_sep = None
    inc_upd = None
    saved = []
    for level in range(4):
        source, block, expand, basis, pivot, couple, ranks, targets = levels[level]
        correction_entries, weight_entries, parts = forward_level(
            source, inc_sep, block, expand, basis, pivot, ranks, bit_counts[level], owners[level]
        )
        saved.append((correction_entries, parts))
        if level < 3:
            update = -outer(weight_entries, couple)
            if inc_upd is not None:
                update = update + inc_upd
            sep_total = levels[level + 1][0].shape[1] * across * groups[level + 1]
            has_update = level + 1 < 3
            stack = extend(update, targets, sep_total, has_update, bit_counts[level + 1], place)
            inc_sep = stack[0]
            inc_upd = stack[1] if has_update else None
    answers = [None, None, None, None]
    parent_stack = None
    for level in (3, 2, 1, 0):
        correction_entries, parts = saved[level]
        couple = levels[level][5]
        expand = levels[level][2]
        targets = levels[level][7]
        x_upd = None
        if level < 3:
            x_upd = fetch(parent_stack, targets, bit_counts[level + 1], place)
        xvals = backward_level(correction_entries, x_upd, couple, expand, parts, bit_counts[level])
        answers[level] = xvals
        if level > 0:
            parent_stack = xvals[None] if x_upd is None else jnp.stack([xvals, x_upd])
    return (answers[0], answers[1], answers[2], answers[3])


def solution(mesh):
    in_specs = (
        P(None, ("leaf", "grid")),
        P(("leaf", "grid"), None),
        P(("leaf", "grid"), None),
        P(("leaf", "grid"), None),
        P(("leaf", "grid")),
        P(("leaf", "grid"), None),
        P(),
        P(("leaf", "grid")),
        P(None, ("leaf", "grid")),
        P(("leaf", "grid"), None),
        P(("leaf", "grid"), None),
        P(("leaf", "grid"), None),
        P(("leaf", "grid")),
        P(("leaf", "grid"), None),
        P(),
        P(("leaf", "grid")),
        P(None, ("leaf", "grid")),
        P(("leaf", "grid"), None),
        P(("leaf", "grid"), None),
        P(("leaf", "grid"), None),
        P(("leaf", "grid")),
        P(("leaf", "grid"), None),
        P(),
        P(("leaf", "grid")),
        P(None, ("leaf", "grid")),
        P(("leaf", "grid"), None),
        P(("leaf", "grid"), None),
        P(("leaf", "grid"), None),
        P(("leaf", "grid")),
        P(),
    )
    out_specs = (
        P(None, ("leaf", "grid")),
        P(None, ("leaf", "grid")),
        P(None, ("leaf", "grid")),
        P(None, ("leaf", "grid")),
    )
    return jax.shard_map(shards, mesh=mesh, in_specs=in_specs, out_specs=out_specs, check_vma=False)
```

profile of v0, /device:TPU:0, one launch (start us, length us, event | category | flops | bytes accessed | tf_op | source)
XLA Modules:
  0.0 397.3 jit_solution(7661426514770940477)
XLA Ops:
  17.3 27.4 %all-reduce.5.cloned.1.call-done = f32[144,128]{1,0:T(8,128)} async-done(((f32[144,128]{1,0:T(8,128)}), f32[144,128]{1,0:T(8,128)}) %all-reduce.5.cloned.1.call-update) | async-done | bytes 73744 | tf_op jit(solution)/shard_map/psum | solution.py:44
  46.1 1.7 scatter_custom_fusion
  48.2 1.9 collective-permute-start
  50.2 2.0 collective-permute-done
  53.4 21.0 %reduce-scatter.4.cloned.1.call-done = f32[2,8,128]{2,1,0:T(8,128)} async-done(((f32[2,8,512]{2,1,0:T(8,128)}), f32[2,8,128]{2,1,0:T(8,128)}) %reduce-scatter.4.cloned.1.call-update) | async-done | bytes 8208 | tf_op jit(solution)/shard_map/reduce_scatter | solution.py:67
  77.7 29.1 %all-reduce.7.cloned.1.call-done = f32[144,128]{1,0:T(8,128)} async-done(((f32[144,128]{1,0:T(8,128)}), f32[144,128]{1,0:T(8,128)}) %all-reduce.7.cloned.1.call-update) | async-done | bytes 73744 | tf_op jit(solution)/shard_map/psum | solution.py:44
  106.8 1.9 collective-permute-start.1
  109.3 2.3 collective-permute-done.1
  114.2 1.5 scatter_custom_fusion.1
  117.0 1.6 copy.75
  118.9 1.8 collective-permute-start.2
  121.1 2.2 collective-permute-done.2
  123.3 1.8 collective-permute-start.3
  125.1 2.2 collective-permute-done.3
  128.0 21.2 %reduce-scatter.6.cloned.1.call-done = f32[2,8,128]{2,1,0:T(8,128)} async-done(((f32[2,8,512]{2,1,0:T(8,128)}), f32[2,8,128]{2,1,0:T(8,128)}) %reduce-scatter.6.cloned.1.call-update) | async-done | bytes 8208 | tf_op jit(solution)/shard_map/reduce_scatter | solution.py:67
  152.4 29.2 %all-reduce.9.cloned.1.call-done = f32[144,128]{1,0:T(8,128)} async-done(((f32[144,128]{1,0:T(8,128)}), f32[144,128]{1,0:T(8,128)}) %all-reduce.9.cloned.1.call-update) | async-done | bytes 73744 | tf_op jit(solution)/shard_map/psum | solution.py:44
  181.6 1.9 collective-permute-start.4
  184.1 2.3 collective-permute-done.4
  187.4 1.8 collective-permute-start.5
  189.9 1.9 collective-permute-done.5
  193.5 1.5 scatter_custom_fusion.2
  196.0 2.7 collective-permute-start.6
  198.7 2.8 collective-permute-done.6
  203.0 1.8 collective-permute-start.7
  205.2 9.0 %collective-permute-done.7 = f32[1,8,1024]{1,2,0:T(8,128)S(1)} collective-permute-done((f32[1,8,1024]{1,2,0:T(8,128)S(1)}, f32[1,8,1024]{1,2,0:T(8,128)S(1)}, u32[]{:S(2)}, u32[]{:S(2)}) %collective-permute-start.7) | collective-permute-done | bytes 32800 | tf_op jit(solution)/shard_map/ppermute | solution.py:16
  214.4 1.7 collective-permute-start.8
  216.7 4.2 %collective-permute-done.8 = f32[1,8,512]{1,2,0:T(8,128)S(1)} collective-permute-done((f32[1,8,512]{1,2,0:T(8,128)S(1)}, f32[1,8,512]{1,2,0:T(8,128)S(1)}, u32[]{:S(2)}, u32[]{:S(2)}) %collective-permute-start.8) | collective-permute-done | bytes 16416 | tf_op jit(solution)/shard_map/ppermute | solution.py:16
  222.3 20.4 %reduce-scatter.8.cloned.1.call-done = f32[1,8,128]{1,2,0:T(8,128)} async-done(((f32[1,8,512]{1,2,0:T(8,128)}), f32[1,8,128]{1,2,0:T(8,128)}) %reduce-scatter.8.cloned.1.call-update) | async-done | bytes 4112 | tf_op jit(solution)/shard_map/reduce_scatter | solution.py:67
  246.3 29.2 %all-reduce.11.cloned.1.call-done = f32[144,128]{1,0:T(8,128)} async-done(((f32[144,128]{1,0:T(8,128)}), f32[144,128]{1,0:T(8,128)}) %all-reduce.11.cloned.1.call-update) | async-done | bytes 73744 | tf_op jit(solution)/shard_map/psum | solution.py:44
  275.5 1.9 collective-permute-start.9
  277.4 3.0 collective-permute-done.9
  281.3 1.8 collective-permute-start.10
  283.1 2.6 collective-permute-done.10
  285.7 2.7 collective-permute-start.11
  288.5 2.5 collective-permute-done.11
  291.4 5.9 %psum.60 = f32[8,128]{1,0:T(8,128)S(1)} all-reduce(f32[8,128]{1,0:T(8,128)S(1)} %fusion.123), channel_id=1, replica_groups=mesh['leaf'=8,'grid'=4] {'grid'}, use_global_device_ids=true, to_apply=%region_10.11 | all-reduce | flops 1024 | bytes 8192 | tf_op jit(solution)/shard_map/psum | solution.py:44
  297.4 1.5 collective-permute-start.12
  298.9 2.1 collective-permute-done.12
  301.0 1.5 collective-permute-start.13
  302.7 1.9 collective-permute-done.13
  304.6 3.0 collective-permute-start.14
  307.8 1.4 collective-permute-done.14
  309.4 5.6 %all-gather = f32[8,512]{1,0:T(8,128)S(1)} all-gather(f32[8,128]{1,0:T(8,128)S(1)} %convolution_add_fusion.3), channel_id=2, replica_groups=mesh['leaf'=8,'grid'=4] {'grid'}, dimensions={1}, use_global_device_ids=true | all-gather | bytes 20480 | tf_op jit(solution)/shard_map/all_gather | solution.py:71
  314.9 1.5 collective-permute-start.15
  316.6 2.1 collective-permute-done.15
  318.7 1.5 collective-permute-start.16
  320.2 2.4 collective-permute-done.16
  322.6 3.0 collective-permute-start.17
  325.6 2.2 collective-permute-done.17
  330.0 5.8 %psum.61 = f32[16,128]{1,0:T(8,128)S(1)} all-reduce(f32[16,128]{1,0:T(8,128)S(1)} %pad_maximum_fusion.6), channel_id=1, replica_groups=mesh['leaf'=8,'grid'=4] {'grid'}, use_global_device_ids=true, to_apply=%region_11.13 | all-reduce | flops 2048 | bytes 16384 | tf_op jit(solution)/shard_map/psum | solution.py:44
  335.8 1.5 collective-permute-start.18
  339.5 1.7 collective-permute-start.19
  346.0 5.5 %all_gather.10 = f32[2,8,512]{2,1,0:T(8,128)S(1)} all-gather(f32[2,8,128]{2,1,0:T(8,128)S(1)} %pad_maximum_fusion.7), channel_id=1, replica_groups=mesh['leaf'=8,'grid'=4] {'grid'}, dimensions={2}, use_global_device_ids=true | all-gather | bytes 40960 | tf_op jit(solution)/shard_map/all_gather | solution.py:71
  351.5 1.5 collective-permute-start.20
  353.2 2.2 collective-permute-done.20
  355.4 1.8 collective-permute-start.21
  357.3 2.4 collective-permute-done.21
  361.3 5.8 %psum.62 = f32[16,128]{1,0:T(8,128)S(1)} all-reduce(f32[16,128]{1,0:T(8,128)S(1)} %pad_maximum_fusion.8), channel_id=1, replica_groups=mesh['leaf'=8,'grid'=4] {'grid'}, use_global_device_ids=true, to_apply=%region_12.14 | all-reduce | flops 2048 | bytes 16384 | tf_op jit(solution)/shard_map/psum | solution.py:44
  367.1 1.5 collective-permute-start.22
  368.6 2.2 collective-permute-done.22
  371.7 5.3 %all_gather.11 = f32[2,8,512]{2,1,0:T(8,128)S(1)} all-gather(f32[2,8,128]{2,1,0:T(8,128)S(1)} %pad_maximum_fusion.9), channel_id=1, replica_groups=mesh['leaf'=8,'grid'=4] {'grid'}, dimensions={2}, use_global_device_ids=true | all-gather | bytes 40960 | tf_op jit(solution)/shard_map/all_gather | solution.py:71
  377.0 1.5 collective-permute-start.23
  378.6 2.3 collective-permute-done.23
  382.5 6.5 %psum.63 = f32[16,128]{1,0:T(8,128)S(1)} all-reduce(f32[16,128]{1,0:T(8,128)S(1)} %pad_maximum_fusion.10), channel_id=1, replica_groups=mesh['leaf'=8,'grid'=4] {'grid'}, use_global_device_ids=true, to_apply=%region_13.15 | all-reduce | flops 2048 | bytes 16384 | tf_op jit(solution)/shard_map/psum | solution.py:44
  (264 shorter events, 54.5 us)
Async XLA Ops:
  7.2 38.5 %copy-start = (f32[256,128]{1,0:T(8,128)S(1)}, f32[256,128]{1,0:T(8,128)}, u32[]{:S(2)}) copy-start(f32[256,128]{1,0:T(8,128)} %param.37) | copy-start | bytes 393220
  7.2 37.5 %all-reduce.5.cloned.1.call-start = ((), (), s32[]{:S(2)}) async-start(), calls=%async_computation.3 | async-start | bytes 147456 | tf_op jit(solution)/shard_map/psum | solution.py:44
  12.1 62.3 %reduce-scatter.4.cloned.1.call-start = ((), (), s32[]{:S(2)}) async-start(), calls=%async_computation.4 | async-start | bytes 40960 | tf_op jit(solution)/shard_map/reduce_scatter | solution.py:67
  14.1 33.9 %copy-start.42 = (s32[256]{0:T(256)}, s32[256]{0:T(256)S(1)}, u32[]{:S(2)}) copy-start(s32[256]{0:T(256)S(1)} %compare_select_fusion) | copy-start | bytes 3076
  14.8 99.4 %copy-start.50 = (s32[128]{0:T(128)}, s32[128]{0:T(128)S(1)}, u32[]{:S(2)}) copy-start(s32[128]{0:T(128)S(1)} %compare_select_fusion.1) | copy-start | bytes 1540
  47.8 65.4 %copy-start.20 = (f32[128,128]{1,0:T(8,128)S(1)}, f32[128,128]{1,0:T(8,128)}, u32[]{:S(2)}) copy-start(f32[128,128]{1,0:T(8,128)} %param.45) | copy-start | bytes 196612
  48.2 4.0 collective-permute-start
  52.8 54.0 %all-reduce.7.cloned.1.call-start = ((), (), s32[]{:S(2)}) async-start(), calls=%async_computation.5 | async-start | bytes 147456 | tf_op jit(solution)/shard_map/psum | solution.py:44
  77.0 72.3 %reduce-scatter.6.cloned.1.call-start = ((), (), s32[]{:S(2)}) async-start(), calls=%async_computation.6 | async-start | bytes 40960 | tf_op jit(solution)/shard_map/reduce_scatter | solution.py:67
  77.7 39.2 %copy-start.34 = (f32[128]{0:T(128)}, f32[128]{0:T(128)S(1)}, u32[]{:S(2)}) copy-start(f32[128]{0:T(128)S(1)} %compare_convert_fusion.4) | copy-start | bytes 1540
  106.8 4.9 %collective-permute-start.1 = (f32[144,128]{1,0:T(8,128)}, f32[144,128]{1,0:T(8,128)S(1)}, u32[]{:S(2)}, u32[]{:S(2)}) collective-permute-start(f32[144,128]{1,0:T(8,128)} %all-reduce.7.cloned.1.call-done), channel_id=1, source_target_pairs={{0,4},{4,0},{8,12},{12,8},{16,20},{20,16},{24,28},{28,24},{1,5},{5... | collective-permute-start | bytes 221192 | tf_op jit(solution)/shard_map/ppermute | solution.py:16
  117.0 75.5 %copy-start.18 = (f32[128,128]{1,0:T(8,128)S(1)}, f32[128,128]{1,0:T(8,128)}, u32[]{:S(2)}) copy-start(f32[128,128]{1,0:T(8,128)} %param.53) | copy-start | bytes 196612
  118.9 4.3 %collective-permute-start.2 = (f32[2,8,1024]{2,1,0:T(8,128)S(1)}, f32[2,8,1024]{2,1,0:T(8,128)S(1)}, u32[]{:S(2)}, u32[]{:S(2)}) collective-permute-start(f32[2,8,1024]{2,1,0:T(8,128)S(1)} %broadcast_select_fusion), channel_id=1, source_target_pairs={{0,8},{4,12},{8,0},{12,4},{16,24},{20,28},{24,16},{28,20},{1,9},{5... | collective-permute-start | bytes 196616 | tf_op jit(solution)/shard_map/ppermute | solution.py:16
  123.3 4.0 %collective-permute-start.3 = (f32[2,8,512]{2,1,0:T(8,128)S(1)}, f32[2,8,512]{2,1,0:T(8,128)S(1)}, u32[]{:S(2)}, u32[]{:S(2)}) collective-permute-start(f32[2,8,512]{2,1,0:T(8,128)S(1)} %slice_select_fusion.3), channel_id=1, source_target_pairs={{0,4},{4,0},{8,12},{12,8},{16,20},{20,16},{24,28},{28,24},{1,5},{5... | collective-permute-start | bytes 98312 | tf_op jit(solution)/shard_map/ppermute | solution.py:16
  125.1 69.9 %copy-start.52 = (s32[128]{0:T(128)}, s32[128]{0:T(128)S(1)}, u32[]{:S(2)}) copy-start(s32[128]{0:T(128)S(1)} %compare_select_fusion.2) | copy-start | bytes 1540
  127.9 53.7 %all-reduce.9.cloned.1.call-start = ((), (), s32[]{:S(2)}) async-start(), calls=%async_computation.7 | async-start | bytes 147456 | tf_op jit(solution)/shard_map/psum | solution.py:44
  151.8 90.8 %reduce-scatter.8.cloned.1.call-start = ((), (), s32[]{:S(2)}) async-start(), calls=%async_computation.8 | async-start | bytes 327680 | tf_op jit(solution)/shard_map/reduce_scatter | solution.py:67
  181.6 4.9 %collective-permute-start.4 = (f32[144,128]{1,0:T(8,128)}, f32[144,128]{1,0:T(8,128)S(1)}, u32[]{:S(2)}, u32[]{:S(2)}) collective-permute-start(f32[144,128]{1,0:T(8,128)} %all-reduce.9.cloned.1.call-done), channel_id=1, source_target_pairs={{0,4},{4,0},{8,12},{12,8},{16,20},{20,16},{24,28},{28,24},{1,5},{5... | collective-permute-start | bytes 221192 | tf_op jit(solution)/shard_map/ppermute | solution.py:16
  187.4 4.4 %collective-permute-start.5 = (f32[144,128]{1,0:T(8,128)S(1)}, f32[144,128]{1,0:T(8,128)S(1)}, u32[]{:S(2)}, u32[]{:S(2)}) collective-permute-start(f32[144,128]{1,0:T(8,128)S(1)} %add.207), channel_id=1, source_target_pairs={{0,8},{4,12},{8,0},{12,4},{16,24},{20,28},{24,16},{28,20},{1,9},{5... | collective-permute-start | bytes 221192 | tf_op jit(solution)/shard_map/ppermute | solution.py:16
  196.0 5.5 %collective-permute-start.6 = (f32[1,8,2048]{2,1,0:T(8,128)}, f32[1,8,2048]{2,1,0:T(8,128)}, u32[]{:S(2)}, u32[]{:S(2)}) collective-permute-start(f32[1,8,2048]{2,1,0:T(8,128)} %copy.65), channel_id=1, source_target_pairs={{0,16},{4,20},{8,24},{12,28},{16,0},{20,4},{24,8},{28,12},{1,17},{... | collective-permute-start | bytes 196616 | tf_op jit(solution)/shard_map/ppermute | solution.py:16
  203.0 11.2 %collective-permute-start.7 = (f32[1,8,1024]{1,2,0:T(8,128)S(1)}, f32[1,8,1024]{1,2,0:T(8,128)S(1)}, u32[]{:S(2)}, u32[]{:S(2)}) collective-permute-start(f32[1,8,1024]{1,2,0:T(8,128)S(1)} %slice_select_fusion.1), channel_id=1, source_target_pairs={{0,8},{4,12},{8,0},{12,4},{16,24},{20,28},{24,16},{28,20},{1,9},{5... | collective-permute-start | bytes 98312 | tf_op jit(solution)/shard_map/ppermute | solution.py:16
  205.1 37.5 %copy-start.17 = (f32[128,128]{1,0:T(8,128)S(1)}, f32[128,128]{1,0:T(8,128)}, u32[]{:S(2)}) copy-start(f32[128,128]{1,0:T(8,128)} %param.57) | copy-start | bytes 196612
  205.1 38.6 %copy-start.15 = (f32[128,256]{1,0:T(8,128)S(1)}, f32[128,256]{1,0:T(8,128)}, u32[]{:S(2)}) copy-start(f32[128,256]{1,0:T(8,128)} %param.59) | copy-start | bytes 393220
  205.1 40.5 %copy-start.58 = (s32[128]{0:T(128)S(1)}, s32[128]{0:T(128)}, u32[]{:S(2)}) copy-start(s32[128]{0:T(128)} %param.47) | copy-start | bytes 1540
  205.1 72.2 %copy-start.53 = (s32[128]{0:T(128)S(1)}, s32[128]{0:T(128)}, u32[]{:S(2)}) copy-start(s32[128]{0:T(128)} %copy-done.52) | copy-start | bytes 1540
  205.1 77.9 %copy-start.51 = (s32[128]{0:T(128)S(1)}, s32[128]{0:T(128)}, u32[]{:S(2)}) copy-start(s32[128]{0:T(128)} %copy-done.50) | copy-start | bytes 1540
  214.3 74.2 %copy-start.59 = (s32[1,2]{1,0:T(1,128)S(1)}, s32[1,2]{1,0:T(1,128)}, u32[]{:S(2)}) copy-start(s32[1,2]{1,0:T(1,128)} %param.61) | copy-start | bytes 28
  214.3 76.8 %copy-start.9 = (f32[128,128]{1,0:T(8,128)S(1)}, f32[128,128]{1,0:T(8,128)}, u32[]{:S(2)}) copy-start(f32[128,128]{1,0:T(8,128)} %param.58) | copy-start | bytes 196612
  214.3 76.8 %copy-start.54 = (f32[128]{0:T(128)S(1)}, f32[128]{0:T(128)}, u32[]{:S(2)}) copy-start(f32[128]{0:T(128)} %param.60) | copy-start | bytes 1540
  214.3 84.6 %copy-start.43 = (s32[256]{0:T(256)S(1)}, s32[256]{0:T(256)}, u32[]{:S(2)}) copy-start(s32[256]{0:T(256)} %copy-done.42) | copy-start | bytes 3076
  214.3 88.2 %copy-start.7 = (f32[144,128]{1,0:T(8,128)S(1)}, f32[144,128]{1,0:T(8,128)}, u32[]{:S(2)}) copy-start(f32[144,128]{1,0:T(8,128)} %copy-done.6) | copy-start | bytes 221188
  214.3 88.2 %copy-start.11 = (f32[128,128]{1,0:T(8,128)S(1)}, f32[128,128]{1,0:T(8,128)}, u32[]{:S(2)}) copy-start(f32[128,128]{1,0:T(8,128)} %param.50) | copy-start | bytes 196612
  214.3 88.2 %copy-start.39 = (f32[128]{0:T(128)S(1)}, f32[128]{0:T(128)}, u32[]{:S(2)}) copy-start(f32[128]{0:T(128)} %copy-done.38) | copy-start | bytes 1540
  214.3 88.2 %copy-start.47 = (f32[128]{0:T(128)S(1)}, f32[128]{0:T(128)}, u32[]{:S(2)}) copy-start(f32[128]{0:T(128)} %param.52) | copy-start | bytes 1540
  214.4 6.4 %collective-permute-start.8 = (f32[1,8,512]{1,2,0:T(8,128)S(1)}, f32[1,8,512]{1,2,0:T(8,128)S(1)}, u32[]{:S(2)}, u32[]{:S(2)}) collective-permute-start(f32[1,8,512]{1,2,0:T(8,128)S(1)} %slice_select_fusion.2), channel_id=1, source_target_pairs={{0,4},{4,0},{8,12},{12,8},{16,20},{20,16},{24,28},{28,24},{1,5},{5... | collective-permute-start | bytes 49160 | tf_op jit(solution)/shard_map/ppermute | solution.py:16
  221.6 53.9 %all-reduce.11.cloned.1.call-start = ((), (), s32[]{:S(2)}) async-start(), calls=%async_computation.9 | async-start | bytes 147456 | tf_op jit(solution)/shard_map/psum | solution.py:44
  244.9 84.3 %copy-start.19 = (f32[128,128]{1,0:T(8,128)S(1)}, f32[128,128]{1,0:T(8,128)}, u32[]{:S(2)}) copy-start(f32[128,128]{1,0:T(8,128)} %param.53) | copy-start | bytes 196612
  245.6 91.7 %copy-start.13 = (f32[128,128]{1,0:T(8,128)S(1)}, f32[128,128]{1,0:T(8,128)}, u32[]{:S(2)}) copy-start(f32[128,128]{1,0:T(8,128)} %param.34) | copy-start | bytes 196612
  245.6 91.7 %copy-start.16 = (f32[144,128]{1,0:T(8,128)S(1)}, f32[144,128]{1,0:T(8,128)}, u32[]{:S(2)}) copy-start(f32[144,128]{1,0:T(8,128)} %all-reduce.5.cloned.1.call-done) | copy-start | bytes 221188
  245.6 91.7 %copy-start.33 = (f32[128]{0:T(128)S(1)}, f32[128]{0:T(128)}, u32[]{:S(2)}) copy-start(f32[128]{0:T(128)} %copy-done.32) | copy-start | bytes 1540
  275.5 4.9 %collective-permute-start.9 = (f32[144,128]{1,0:T(8,128)}, f32[144,128]{1,0:T(8,128)S(1)}, u32[]{:S(2)}, u32[]{:S(2)}) collective-permute-start(f32[144,128]{1,0:T(8,128)} %all-reduce.11.cloned.1.call-done), channel_id=1, source_target_pairs={{0,4},{4,0},{8,12},{12,8},{16,20},{20,16},{24,28},{28,24},{1,5},{5... | collective-permute-start | bytes 221192 | tf_op jit(solution)/shard_map/ppermute | solution.py:16
  281.3 63.6 %copy-start.23 = (f32[128,128]{1,0:T(8,128)S(1)}, f32[128,128]{1,0:T(8,128)}, u32[]{:S(2)}) copy-start(f32[128,128]{1,0:T(8,128)} %param.49) | copy-start | bytes 196612
  281.3 4.4 %collective-permute-start.10 = (f32[144,128]{1,0:T(8,128)S(1)}, f32[144,128]{1,0:T(8,128)S(1)}, u32[]{:S(2)}, u32[]{:S(2)}) collective-permute-start(f32[144,128]{1,0:T(8,128)S(1)} %add.219), channel_id=1, source_target_pairs={{0,8},{4,12},{8,0},{12,4},{16,24},{20,28},{24,16},{28,20},{1,9},{5... | collective-permute-start | bytes 221192 | tf_op jit(solution)/shard_map/ppermute | solution.py:16
  285.7 67.3 %copy-start.5 = (f32[144,128]{1,0:T(8,128)S(1)}, f32[144,128]{1,0:T(8,128)}, u32[]{:S(2)}) copy-start(f32[144,128]{1,0:T(8,128)} %copy-done.4) | copy-start | bytes 221188
  285.7 67.3 %copy-start.12 = (f32[128,128]{1,0:T(8,128)S(1)}, f32[128,128]{1,0:T(8,128)}, u32[]{:S(2)}) copy-start(f32[128,128]{1,0:T(8,128)} %param.42) | copy-start | bytes 196612
  285.7 67.3 %copy-start.35 = (f32[128]{0:T(128)S(1)}, f32[128]{0:T(128)}, u32[]{:S(2)}) copy-start(f32[128]{0:T(128)} %copy-done.34) | copy-start | bytes 1540
  285.7 67.3 %copy-start.48 = (f32[128]{0:T(128)S(1)}, f32[128]{0:T(128)}, u32[]{:S(2)}) copy-start(f32[128]{0:T(128)} %param.44) | copy-start | bytes 1540
  285.7 5.3 %collective-permute-start.11 = (f32[144,128]{1,0:T(8,128)S(1)}, f32[144,128]{1,0:T(8,128)S(1)}, u32[]{:S(2)}, u32[]{:S(2)}) collective-permute-start(f32[144,128]{1,0:T(8,128)S(1)} %add.220), channel_id=1, source_target_pairs={{0,16},{4,20},{8,24},{12,28},{16,0},{20,4},{24,8},{28,12},{1,17},{... | collective-permute-start | bytes 221192 | tf_op jit(solution)/shard_map/ppermute | solution.py:16
  297.4 3.6 collective-permute-start.12
  301.0 3.6 collective-permute-start.13
  304.6 4.6 %collective-permute-start.14 = (f32[8,128]{1,0:T(8,128)S(1)}, f32[8,128]{1,0:T(8,128)S(1)}, u32[]{:S(2)}, u32[]{:S(2)}) collective-permute-start(f32[8,128]{1,0:T(8,128)S(1)} %add.224), channel_id=1, source_target_pairs={{0,16},{4,20},{8,24},{12,28},{16,0},{20,4},{24,8},{28,12},{1,17},{... | collective-permute-start | bytes 12296 | tf_op jit(solution)/shard_map/ppermute | solution.py:16
  309.4 50.4 %copy-start.29 = (f32[8,128]{1,0:T(8,128)}, f32[8,128]{1,0:T(8,128)S(1)}, u32[]{:S(2)}) copy-start(f32[8,128]{1,0:T(8,128)S(1)} %convolution_add_fusion.3) | copy-start | bytes 12292
  314.9 3.7 collective-permute-start.15
  318.7 3.9 collective-permute-start.16
  322.6 5.2 %collective-permute-start.17 = (f32[1,8,2048]{2,1,0:T(8,128)S(1)}, f32[1,8,2048]{2,1,0:T(8,128)S(1)}, u32[]{:S(2)}, u32[]{:S(2)}) collective-permute-start(f32[1,8,2048]{2,1,0:T(8,128)S(1)} %maximum_select_fusion.2), channel_id=1, source_target_pairs={{0,16},{4,20},{8,24},{12,28},{16,0},{20,4},{24,8},{28,12},{1,17},{... | collective-permute-start | bytes 196616 | tf_op jit(solution)/shard_map/ppermute | solution.py:16
  328.5 42.3 %copy-start.37 = (f32[128]{0:T(128)S(1)}, f32[128]{0:T(128)}, u32[]{:S(2)}) copy-start(f32[128]{0:T(128)} %copy-done.36) | copy-start | bytes 1540
  328.5 42.7 %copy-start.25 = (f32[128,128]{1,0:T(8,128)S(1)}, f32[128,128]{1,0:T(8,128)}, u32[]{:S(2)}) copy-start(f32[128,128]{1,0:T(8,128)} %param.41) | copy-start | bytes 196612
  335.8 3.7 collective-permute-start.18
  339.5 3.7 collective-permute-start.19
  346.0 35.3 %copy-start.30 = (f32[8,128]{1,0:T(8,128)}, f32[8,128]{1,0:T(8,128)S(1)}, u32[]{:S(2)}) copy-start(f32[8,128]{1,0:T(8,128)S(1)} %convolution_add_fusion.2) | copy-start | bytes 12292
  351.5 3.9 collective-permute-start.20
  355.4 4.3 %collective-permute-start.21 = (f32[2,8,1024]{2,1,0:T(8,128)S(1)}, f32[2,8,1024]{2,1,0:T(8,128)S(1)}, u32[]{:S(2)}, u32[]{:S(2)}) collective-permute-start(f32[2,8,1024]{2,1,0:T(8,128)S(1)} %maximum_select_fusion.4), channel_id=1, source_target_pairs={{0,8},{4,12},{8,0},{12,4},{16,24},{20,28},{24,16},{28,20},{1,9},{5... | collective-permute-start | bytes 196616 | tf_op jit(solution)/shard_map/ppermute | solution.py:16
  367.1 3.7 collective-permute-start.22
  377.0 3.9 collective-permute-start.23
  (27 other events, 445.1 us)
Sparse Core Ops, SparseCore 0:
  12.2 32.3 all-reduce.4
  52.9 21.4 reduce-scatter.3
  77.1 29.6 all-reduce.6
  128.0 21.1 reduce-scatter.5
  151.9 29.6 all-reduce.8
  221.7 20.8 reduce-scatter.7
  245.8 29.6 all-reduce.10
where the time goes:
time: 398 us; the launch traced here: 397 us
  waiting for transfers between devices  239 us (60%)
  starting transfers between devices  45.5 us (11%)
  blocking collectives  40.3 us (10%)
  matrix products  24 us (6%)
  other arithmetic  20.3 us (5%)
  between operations  15.1 us (4%)
  local copies, waits for them, and re-layouts  13.5 us (3%)
    psum x4, waiting for transfers between devices, paired_total(): summed = lax.psum(partial_value, 'grid')  115 us
    reduce_scatter x3, waiting for transfers between devices, group_extend(): return lax.psum_scatter(stack, 'grid', scatter_dimension=2, tiled=True)  62.6 us
    ppermute x24, waiting for transfers between devices, from_partner(): return lax.ppermute(value, axis, pairs)  61 us
    ppermute x24, starting transfers between devices, from_partner(): return lax.ppermute(value, axis, pairs)  45.2 us
    psum x4, blocking collectives, paired_total(): summed = lax.psum(partial_value, 'grid')  24 us
    all_gather x3, blocking collectives, group_fetch(): current = lax.all_gather(stack, 'grid', axis=2, tiled=True)  16.4 us
    dot_general x18, matrix products, mult(): jnp.dot(left, right, precision=HIGH_PRECISION, preferred_element_type=jnp...  8.73 us
  transfers between devices with their start and end apart: 31, of which 31 were waited for; matrix products, arithmetic and copies ran while one was open for 3% of the time, Pallas kernels for 0%

commit v1 on v0

v1 whole, which is shorter than its diff:
```python
import functools

import jax
import jax.numpy as jnp
from jax import lax
from jax.experimental import pallas as pl
from jax.experimental.pallas import tpu as pltpu
from jax.sharding import PartitionSpec as P

RANK = 128
LANES = 128
MESH = pl.DeviceIdType.MESH
HIGHEST = lax.Precision.HIGHEST
F32 = jnp.float32
BF16 = jnp.bfloat16


def dot(a, b, ca, cb, precision=HIGHEST):
    return lax.dot_general(
        a, b, (((ca,), (cb,)), ((), ())), precision=precision, preferred_element_type=F32
    )


def mult(a, b):
    return dot(a, b, 1, 0)


def outer(a, b):
    return dot(a, b, 1, 1)


def inner(a, b):
    return dot(a, b, 0, 0)


def split3(x):
    hi = x.astype(BF16).astype(F32)
    rest = x - hi
    mid = rest.astype(BF16).astype(F32)
    return jnp.concatenate([hi, mid, rest - mid], axis=0).astype(BF16)


def select(x, onehot, cb):
    out = dot(split3(x), onehot, 1, cb, lax.Precision.DEFAULT)
    n = x.shape[0]
    return out[:n] + out[n : 2 * n] + out[2 * n :]


def kernel(cfg, *refs):
    leaves, across, size, ups, count = cfg
    total_devices = leaves * across
    (src, blk, exp, bas, piv, rnk) = [refs[4 * i : 4 * i + 4] for i in range(6)]
    cpl = refs[24:27]
    tgt = refs[27:30]
    outs = refs[30:34]
    (f1, f2, f3, f4, f5, b1, b2, b3) = refs[34:42]
    fwd = (f1, f2, f3)
    bwd = (b3, b2, b1)
    perm_buf = refs[42:45]
    recv_c = refs[45:48]
    cross_p = refs[48:51]
    rs_buf = refs[51:54]
    cross_all = refs[54:57]
    tg_buf = (None,) + tuple(refs[57:59])
    bot = (None,) + tuple(refs[59:61])
    fts = refs[61:-5]
    ft = (None, fts[0], fts[-1])
    gt = refs[-5:-2]
    send_sem, recv_sem = refs[-2:]

    me = lax.axis_index("leaf") * across + lax.axis_index("grid")
    pending = []

    def where(peer):
        return (peer // across, peer % across)

    def remote(a, b, sem, peer):
        return pltpu.make_async_remote_copy(
            src_ref=a,
            dst_ref=b,
            send_sem=send_sem.at[sem],
            recv_sem=recv_sem.at[sem],
            device_id=where(peer),
            device_id_type=MESH,
        )

    def wait_for(part, sem):
        pltpu.make_async_copy(part, part, sem).wait()

    def send_all(buf, group, sem):
        idx = me % group
        base = me - idx

        def body(k, carry):
            peer = base + (idx + k) % group
            remote(buf.at[idx], buf.at[idx], sem, peer).start()
            return carry

        lax.fori_loop(1, group, body, 0)
        pending.append((buf.at[pl.ds(0, group - 1)], sem))

    def arrive(buf, group, sem):
        wait_for(buf.at[pl.ds(0, group - 1)], recv_sem.at[sem])

    barrier = pltpu.get_barrier_semaphore()

    def greet(k, carry):
        pl.semaphore_signal(
            barrier, inc=1, device_id=where((me + k) % total_devices), device_id_type=MESH
        )
        return carry

    lax.fori_loop(1, total_devices, greet, 0)

    col = lax.broadcasted_iota(jnp.int32, (count, RANK), 1)

    def mask(level, front, which):
        return (col < rnk[level][front, which]).astype(F32)

    def local_forward(level, b):
        local = mult(b, blk[level][...])
        bq = mult(b, bas[level][:, :RANK])
        lv = mult(local, bas[level][:, RANK:]) if level < 3 else None
        return local, bq, lv

    b = src[0][...]
    local, bq, lv = local_forward(0, b)
    idx = me % size[1]
    f1[idx] = jnp.concatenate([bq, lv], axis=0)
    for level in range(3):
        cross_p[level][...] = inner(exp[level][...], bas[level][:, RANK:])
    pl.semaphore_wait(barrier, total_devices - 1)
    send_all(f1, size[1], 0)

    parts_of = [min(size[level], 16) for level in range(3)]
    for level in range(3):
        g = size[level]
        p = parts_of[level]
        rp = RANK // p
        idx = me % g
        base = me - idx
        sem = 8 + level
        start = 1 if g == p else 0

        def scatter(k, carry, level=level, g=g, p=p, rp=rp, idx=idx, base=base, sem=sem):
            q = (idx + k) % p

            def go():
                rows = pl.ds(pl.multiple_of(q * rp, 8), rp)
                remote(cross_p[level].at[rows], rs_buf[level].at[idx], sem, base + q).start()

            if g == p:
                go()
            else:
                pl.when(q != idx)(go)
            return carry

        lax.fori_loop(start, p, scatter, 0)

        def keep(level=level, rp=rp, idx=idx):
            rows = pl.ds(pl.multiple_of(idx * rp, 8), rp)
            rs_buf[level][idx] = cross_p[level][rows, :]

        if g == p:
            keep()
        else:
            pl.when(idx < p)(keep)

    for level in (1, 2):
        gp = size[level + 1]
        tg_buf[level][me % gp] = jnp.broadcast_to(tgt[level][...], (8, LANES)).astype(F32)
        send_all(tg_buf[level], gp, 14 + level)

    for level in range(3):
        gp = size[level + 1]
        u = ups[level]
        cap = perm_buf[level].shape[1]
        sep = gp * LANES
        t = tgt[level][...]
        upd = t >= sep
        rel = jnp.where(upd, t - sep, t)
        dst = rel // LANES
        low = rel % LANES + jnp.where(upd, LANES, 0)
        ri = lax.broadcasted_iota(jnp.int32, (u, u), 0)
        ci = lax.broadcasted_iota(jnp.int32, (u, u), 1)
        dst_f = dst.astype(F32)
        dst_c = jnp.sum(jnp.where(ri == ci, jnp.broadcast_to(dst_f, (u, u)), 0.0), axis=1, keepdims=True)
        rank = jnp.sum(
            jnp.where((dst_c == dst_f) & (ri < ci), 1.0, 0.0), axis=0, keepdims=True
        ).astype(jnp.int32)
        pos = dst * cap + rank
        slots = gp * cap
        si = lax.broadcasted_iota(jnp.int32, (slots, u), 0)
        hit = (si == pos).astype(F32)
        moved = mult(hit, cpl[level][...])
        lowc = jnp.sum(hit * low.astype(F32), axis=1, keepdims=True)
        both = jnp.concatenate([moved, jnp.broadcast_to(lowc, (slots, LANES))], axis=1)
        perm_buf[level][...] = both.reshape(gp, cap, 2 * LANES)
        idx = me % gp
        base = me - idx
        recv_c[level][idx] = perm_buf[level][idx]

        def ship(k, carry, level=level, gp=gp, idx=idx, base=base):
            q = (idx + k) % gp
            remote(perm_buf[level].at[q], recv_c[level].at[idx], 11 + level, base + q).start()
            return carry

        lax.fori_loop(1, gp, ship, 0)
        pending.append((perm_buf[level].at[pl.ds(0, gp - 1)], 11 + level))

    for level in range(3):
        g = size[level]
        gp = size[level + 1]
        p = parts_of[level]
        rp = RANK // p
        nch = gp // g
        idx = me % g
        place = me % gp
        base = me - place
        sem = 17 + level
        slot = place // g * p + idx

        def gather(level=level, g=g, gp=gp, idx=idx, place=place, base=base, sem=sem, slot=slot):
            wait_for(rs_buf[level].at[pl.ds(0, g - 1)], recv_sem.at[8 + level])
            cross_all[level][slot] = jnp.sum(rs_buf[level][...], axis=0)

            def body(k, carry):
                peer = base + (place + k) % gp
                part = cross_all[level].at[slot]
                remote(part, part, sem, peer).start()
                return carry

            lax.fori_loop(1, gp, body, 0)

        if g == p:
            gather()
        else:
            pl.when(idx < p)(gather)

    late = total_devices > 64

    def build_ft(level):
        chunk = LANES
        t = tgt[level][...]
        ri = lax.broadcasted_iota(jnp.int32, (chunk, LANES), 0)

        def fill_ft(j, carry):
            rows = pl.ds(pl.multiple_of(j * chunk, chunk), chunk)
            ft[level][rows, :] = (ri + j * chunk == t).astype(F32).astype(BF16)
            return carry

        lax.fori_loop(0, ft[level].shape[0] // chunk, fill_ft, 0)

    for level in (1, 2):
        gp = size[level + 1]
        place = me % gp
        rows = bot[level].shape[0]
        ri = lax.broadcasted_iota(jnp.int32, (rows, LANES), 0)
        arrive(tg_buf[level], gp, 14 + level)
        mine = jnp.where(ri < LANES, place * LANES + ri, (gp + place - 1) * LANES + ri).astype(F32)

        def fill(j, carry, level=level, mine=mine):
            t = tg_buf[level][j][0:1, :]
            lanes = pl.ds(pl.multiple_of(j * LANES, LANES), LANES)
            bot[level][:, lanes] = (mine == t).astype(F32).astype(BF16)
            return carry

        lax.fori_loop(0, gp, fill, 0)
        if not late:
            build_ft(level)

    def build_gt(level):
        g = size[level]
        gp = size[level + 1]
        cap = recv_c[level].shape[1]
        nch = gp // g
        rows = gt[level].shape[1]
        arrive(recv_c[level], gp, 11 + level)
        slots = g * cap
        lane = lax.broadcasted_iota(jnp.int32, (slots, rows), 1).astype(F32)
        for child in range(nch):
            got = recv_c[level][child * g : (child + 1) * g].reshape(slots, 2 * LANES)
            ot = (lane == got[:, LANES : LANES + 1]).astype(F32)
            gt[level][child * RANK : (child + 1) * RANK, :] = inner(got[:, :LANES], ot)

    def arrive_cross(level):
        g = size[level]
        p = parts_of[level]
        n = size[level + 1] // g * p
        sem = 17 + level
        if g == p:
            wait_for(cross_all[level].at[pl.ds(0, n - 1)], recv_sem.at[sem])
        else:
            idx = me % g
            pl.when(idx < p)(lambda: wait_for(cross_all[level].at[pl.ds(0, n - 1)], recv_sem.at[sem]))
            pl.when(idx >= p)(lambda: wait_for(cross_all[level].at[pl.ds(0, n)], recv_sem.at[sem]))

    def cross_of(level, child):
        p = parts_of[level]
        return cross_all[level][pl.ds(child * p, p)].reshape(RANK, RANK)

    saved = []
    z_total = []
    inc_upd = None
    for level in range(3):
        g = size[level]
        gp = size[level + 1]
        nch = gp // g
        place = me % gp
        parent = me // gp
        child_me = place // g
        build_gt(level)
        arrive_cross(level)
        buf = fwd[level]
        arrive(buf, gp, level)
        ws = []
        for child in range(nch):
            tot = jnp.sum(buf[child * g : (child + 1) * g, : 2 * count, :], axis=0)
            front = parent * nch + child
            hq = tot[:count] * mask(level, front, 0)
            cross = cross_of(level, child)
            ws.append((tot[count:] + mult(hq, cross)) * mask(level, front, 1))
        inc = -mult(jnp.concatenate(ws, axis=1), gt[level][...])
        if inc_upd is not None:
            rows = jnp.concatenate([buf[j, 2 * count : 3 * count, :] for j in range(gp)], axis=1)
            inc = inc + select(rows, bot[level][...], 1)
            below = size[level - 1]
            first = place // below * below
            z_total.append(jnp.sum(buf[pl.ds(first, below), 3 * count : 4 * count, :], axis=0))
        bn = src[level + 1][...] + inc[:, :LANES]
        local_n, bq_n, lv_n = local_forward(level + 1, bn)
        own = jnp.sum(buf[pl.ds(child_me * g, g), :count, :], axis=0)
        hq = own * mask(level, me // g, 0)
        y = local + outer(hq, exp[level][...])
        z = y * piv[level][...]
        saved.append(z)
        zp = mult(z, exp[level][...])
        if level < 2:
            inc_upd = inc[:, LANES:]
            nxt = fwd[level + 1]
            gn = size[level + 2]
            nxt[me % gn] = jnp.concatenate([bq_n, lv_n, inc_upd, zp], axis=0)
            send_all(nxt, gn, level + 1)
        else:
            f4[me % gp] = jnp.concatenate([bq_n, zp], axis=0)
            send_all(f4, gp, 3)
        local = local_n

    top = size[3]
    place = me % top
    arrive(f4, top, 3)
    tot = jnp.sum(f4[:, :count, :], axis=0)
    below = size[2]
    z_total.append(jnp.sum(f4[pl.ds(place // below * below, below), count:, :], axis=0))
    hq = tot * mask(3, 0, 0)
    z = (local + outer(hq, exp[3][...])) * piv[3][...]
    f5[place] = mult(z, exp[3][...])
    send_all(f5, top, 4)
    base_x = outer(z, blk[3][...])
    arrive(f5, top, 4)
    rp_total = jnp.sum(f5[...], axis=0) * mask(3, 0, 0)
    x = base_x + outer(rp_total, bas[3][:, :RANK])
    outs[3][...] = x

    xu = None
    for level in (2, 1, 0):
        g = size[level]
        gp = size[level + 1]
        nch = gp // g
        place = me % gp
        child_me = place // g
        buf = bwd[level]
        full = x if xu is None else jnp.concatenate([x, xu], axis=1)
        sp = outer(full, gt[level][...])
        pieces = [sp[:, c * RANK : (c + 1) * RANK] for c in range(nch)]
        if level > 0:
            pieces = pieces + ([x] if xu is None else [x, xu])
        buf[place] = jnp.concatenate(pieces, axis=0)
        send_all(buf, gp, 5 + (2 - level))
        arrive(buf, gp, 5 + (2 - level))
        rows = pl.ds(pl.multiple_of(child_me * count, count), count)
        s = jnp.sum(buf[:, rows, :], axis=0) * mask(level, me // g, 1)
        if level > 0:
            o = nch * count
            blocks = [buf[j, o : o + count, :] for j in range(gp)]
            if xu is not None:
                blocks += [buf[j, o + count : o + 2 * count, :] for j in range(gp)]
            if late:
                build_ft(level)
            xu = select(jnp.concatenate(blocks, axis=1), ft[level][...], 0)
        r = saved[level] - outer(s, bas[level][:, RANK:])
        proj = (z_total[level] - outer(s, cross_of(level, child_me))) * mask(level, me // g, 0)
        x = outer(r, blk[level][...]) + outer(proj, bas[level][:, :RANK])
        outs[level][...] = x

    for part, sem in pending:
        wait_for(part, send_sem.at[sem])
    for level in range(3):
        g = size[level]
        gp = size[level + 1]
        p = parts_of[level]
        rp = RANK // p
        n = gp // g * p
        idx = me % g

        def rs_done(pieces, level=level, rp=rp):
            wait_for(cross_p[level].at[pl.ds(0, pieces * rp)], send_sem.at[8 + level])

        def ag_done(level=level, g=g, p=p, n=n):
            for _ in range(g // p - 1):
                wait_for(cross_all[level].at[pl.ds(0, n)], send_sem.at[17 + level])
            wait_for(cross_all[level].at[pl.ds(0, n - 1)], send_sem.at[17 + level])

        if g == p:
            rs_done(p - 1)
            ag_done()
        else:
            pl.when(idx < p)(functools.partial(rs_done, p - 1))
            pl.when(idx >= p)(functools.partial(rs_done, p))
            pl.when(idx < p)(ag_done)


def solution(mesh):
    leaves, across = mesh.shape["leaf"], mesh.shape["grid"]

    def shards(*args):
        levels = [args[8 * i : 8 * i + 8] for i in range(3)]
        root = args[24:30]
        (sl, bl, el, qs, pv, cl, rk, tg) = zip(*levels)
        src = list(sl) + [root[0]]
        blk = list(bl) + [root[1]]
        exp = list(el) + [root[2]]
        bas = list(qs) + [root[3]]
        piv = [v.reshape(1, -1) for v in list(pv) + [root[4]]]
        rnk = list(rk) + [root[5]]
        tgt = [t.reshape(1, -1) for t in tg]
        count = src[0].shape[0]
        ups = [t.shape[1] for t in tgt]
        fronts = [r.shape[0] for r in rnk]
        size = [leaves * across // f for f in fronts]
        for v in src:
            assert v.shape[1] == LANES
        vm = lambda *s: pltpu.VMEM(s, F32)
        nch = [size[i + 1] // size[i] for i in range(3)]
        cap = [max(8, -(-ups[i] // size[i + 1])) for i in range(3)]
        rows = [2 * LANES, 2 * LANES, LANES]
        parts = [min(size[i], 16) for i in range(3)]
        scratch = [
            vm(size[1], 2 * count, LANES),
            vm(size[2], 4 * count, LANES),
            vm(size[3], 4 * count, LANES),
            vm(size[3], 2 * count, LANES),
            vm(size[3], count, LANES),
            vm(size[3], (nch[2] + 1) * count, LANES),
            vm(size[2], (nch[1] + 2) * count, LANES),
            vm(size[1], nch[0] * count, LANES),
        ]
        scratch += [vm(size[i + 1], cap[i], 2 * LANES) for i in range(3)] * 2
        scratch += [vm(RANK, RANK) for i in range(3)]
        scratch += [vm(size[i], RANK // parts[i], RANK) for i in range(3)]
        scratch += [vm(nch[i] * parts[i], RANK // parts[i], RANK) for i in range(3)]
        scratch += [vm(size[i + 1], 8, LANES) for i in (1, 2)]
        scratch += [pltpu.VMEM((rows[i], size[i + 1] * LANES), BF16) for i in (1, 2)]
        fts = (1, 2) if leaves * across <= 64 else (1,)
        scratch += [pltpu.VMEM((size[i + 1] * rows[i], LANES), BF16) for i in fts]
        scratch += [vm(nch[i] * RANK, rows[i]) for i in range(3)]
        scratch += [pltpu.SemaphoreType.DMA((20,)), pltpu.SemaphoreType.DMA((20,))]
        vspec = pl.BlockSpec(memory_space=pltpu.VMEM)
        sspec = pl.BlockSpec(memory_space=pltpu.SMEM)
        return pl.pallas_call(
            functools.partial(kernel, (leaves, across, size, ups, count)),
            out_shape=[jax.ShapeDtypeStruct(v.shape, F32) for v in src],
            in_specs=[vspec] * 20 + [sspec] * 4 + [vspec] * 6,
            out_specs=[vspec] * 4,
            scratch_shapes=scratch,
            compiler_params=pltpu.CompilerParams(
                collective_id=0, has_side_effects=True, vmem_limit_bytes=60 * 1024 * 1024
            ),
        )(*src, *blk, *exp, *bas, *piv, *rnk, *cl, *tgt)

    spread = ("leaf", "grid")
    level = (P(None, spread), P(spread, None), P(spread, None), P(spread, None), P(spread))
    mid = level + (P(spread, None), P(), P(spread))
    return jax.shard_map(
        shards,
        mesh=mesh,
        in_specs=mid * 3 + level + (P(),),
        out_specs=(P(None, spread),) * 4,
        check_vma=False,
    )
```

time: 398 us -> 92.3 us (0.23)
  waiting for transfers between devices: 239 us -> 0 us
  Pallas kernels: 0 us -> 86.1 us
  starting transfers between devices: 45.5 us -> 0 us
  blocking collectives: 40.3 us -> 0 us
  matrix products: 24 us -> 0 us
  other arithmetic: 20.3 us -> 0 us
  between operations: 15.1 us -> 0.66 us
  local copies, waits for them, and re-layouts: 13.5 us -> 5.31 us
    psum x4 -> x0, waiting for transfers between devices: 115 us -> none  [paired_total(): summed = lax.psum(partial_value, 'grid')]
    pallas_call x0 -> x1, Pallas kernels: none -> 86.1 us  [shards(): pl.pallas_call(functools.partial(kernel, (leaves, across, size, ups, coun...]
    reduce_scatter x3 -> x0, waiting for transfers between devices: 62.6 us -> none  [group_extend(): return lax.psum_scatter(stack, 'grid', scatter_dimension=2, tiled=True)]
    ppermute x24 -> x0, waiting for transfers between devices: 61 us -> none  [from_partner(): return lax.ppermute(value, axis, pairs)]
    ppermute x24 -> x0, starting transfers between devices: 45.2 us -> none  [from_partner(): return lax.ppermute(value, axis, pairs)]
    dot_general x47 -> x0, matrix products: 24 us -> none  [the longest x18 8.73 us: mult(): jnp.dot(left, right, precision=HIGH_PRECISION, preferred_element_type=jnp...]
    psum x4 -> x0, blocking collectives: 24 us -> none  [paired_total(): summed = lax.psum(partial_value, 'grid')]
    all_gather x3 -> x0, blocking collectives: 16.4 us -> none  [group_fetch(): current = lax.all_gather(stack, 'grid', axis=2, tiled=True)]
  transfers between devices with their start and end apart: 31 -> 0, of which waited for: 31 -> 0; matrix products, arithmetic and copies ran while one was open for 3% -> 0% of each run, Pallas kernels for 0% -> 0%
where the time goes in v1:
time: 92.3 us; the launch traced here: 92 us
  Pallas kernels  86.1 us (93%)
  local copies, waits for them, and re-layouts  5.31 us (6%)
    pallas_call x1, Pallas kernels, shards(): pl.pallas_call(functools.partial(kernel, (leaves, across, size, ups, coun...  86.1 us
    unnamed x18, local copies, waits for them, and re-layouts  5.31 us

profile of v1, /device:TPU:0, one launch (start us, length us, event | category | flops | bytes accessed | tf_op | source)
XLA Modules:
  0.0 92.0 jit_solution(4035082522572716568)
XLA Ops:
  0.6 0.0 copy-start.4
  0.6 0.7 copy-done.4
  1.3 0.0 copy-start.5
  1.3 0.7 copy.35.refs_21_
  2.0 0.0 copy-done.5
  2.0 0.7 copy.34.refs_20_
  2.7 86.1 %shard_map.309 = (f32[8,128]{1,0:T(8,128)}, f32[8,128]{1,0:T(8,128)}, f32[8,128]{1,0:T(8,128)}, f32[8,128]{1,0:T(8,128)}) custom-call(f32[8,128]{1,0:T(8,128)} %refs_0_.1, f32[8,128]{1,0:T(8,128)} %refs_1_.1, f32[8,128]{1,0:T(8,128)} %refs_2_.1, f32[8,128]{1,0:T(8,128)} %refs_3_.1, f32[128,128]{1,0:T(8,128)} %refs_4_.1, f32[128,128]{1,0:T(8,128)} %refs_5_.1, ...), custom_call_target="tpu_custom_call" | custom-call | tf_op jit(solution)/shard_map/pallas_call | solution.py:470
  88.7 0.0 copy-start.3
  88.7 0.7 copy-done.3
  89.4 0.0 copy-start.2
  89.4 0.6 copy.40
  90.0 0.1 copy-done.2
  90.1 0.0 copy-start.1
  90.1 0.6 copy.41
  90.7 0.1 copy-done.1
  90.8 0.0 copy-start
  90.8 0.6 copy.42
  91.4 0.1 copy-done
  91.4 0.6 copy.43
Async XLA Ops:
  0.6 0.7 copy-start.4
  1.3 0.7 copy-start.5
  88.7 0.7 copy-start.3
  89.4 0.7 copy-start.2
  90.1 0.7 copy-start.1
  90.8 0.7 copy-start

commit v2 on v1

v2 whole, which is shorter than its diff:
```python
import functools

import jax
import jax.numpy as jnp
from jax import lax
from jax.experimental import pallas as pl
from jax.experimental.pallas import tpu as pltpu
from jax.sharding import PartitionSpec as P

RANK = 128
LANES = 128
MESH = pl.DeviceIdType.MESH
HIGHEST = lax.Precision.HIGHEST
F32 = jnp.float32
BF16 = jnp.bfloat16


def dot(a, b, ca, cb, precision=HIGHEST):
    return lax.dot_general(
        a, b, (((ca,), (cb,)), ((), ())), precision=precision, preferred_element_type=F32
    )


def mult(a, b):
    return dot(a, b, 1, 0)


def outer(a, b):
    return dot(a, b, 1, 1)


def inner(a, b):
    return dot(a, b, 0, 0)


def split3(x):
    hi = x.astype(BF16).astype(F32)
    rest = x - hi
    mid = rest.astype(BF16).astype(F32)
    return jnp.concatenate([hi, mid, rest - mid], axis=0).astype(BF16)


def select(x, onehot, cb):
    out = dot(split3(x), onehot, 1, cb, lax.Precision.DEFAULT)
    n = x.shape[0]
    return out[:n] + out[n : 2 * n] + out[2 * n :]


def kernel(cfg, names, *refs):
    leaves, across, size, ups, count, caps = cfg
    total_devices = leaves * across
    (src, blk, exp, bas, piv, rnk) = [refs[4 * i : 4 * i + 4] for i in range(6)]
    cpl = refs[24:27]
    tgt = refs[27:30]
    outs = refs[30:34]
    m = dict(zip(names, refs[34:-2]))
    send_sem, recv_sem = refs[-2:]
    sems = {}

    me = lax.axis_index("leaf") * across + lax.axis_index("grid")
    plane = size[1]
    planes = total_devices // plane
    spot = me % plane
    layer = me // plane
    late = total_devices > 64
    pending = []

    def where(peer):
        return (peer // across, peer % across)

    def sem_of(name):
        return sems.setdefault(name, len(sems))

    def remote(a, b, sem, peer):
        return pltpu.make_async_remote_copy(
            src_ref=a,
            dst_ref=b,
            send_sem=send_sem.at[sem],
            recv_sem=recv_sem.at[sem],
            device_id=where(peer),
            device_id_type=MESH,
        )

    def wait_for(part, sem):
        pltpu.make_async_copy(part, part, sem).wait()

    def send_each(source, dest, group, name, stride=1):
        idx = me // stride % group
        base = me - idx * stride
        sem = sem_of(name)

        def body(k, carry):
            q = (idx + k) % group
            remote(source(q), dest(idx), sem, base + q * stride).start()
            return carry

        lax.fori_loop(1, group, body, 0)

    def send_all(name, group, stride=1):
        buf = m[name]
        idx = me // stride % group
        send_each(lambda q: buf.at[idx], lambda i: buf.at[i], group, name, stride)
        pending.append((buf.at[pl.ds(0, group - 1)], sem_of(name)))

    def arrive(name, group):
        wait_for(m[name].at[pl.ds(0, group - 1)], recv_sem.at[sem_of(name)])

    barrier = pltpu.get_barrier_semaphore()

    def greet(k, carry):
        pl.semaphore_signal(
            barrier, inc=1, device_id=where((me + k) % total_devices), device_id_type=MESH
        )
        return carry

    lax.fori_loop(1, total_devices, greet, 0)

    col = lax.broadcasted_iota(jnp.int32, (count, RANK), 1)

    def mask(level, front, which):
        return (col < rnk[level][front, which]).astype(F32)

    def local_forward(level, b):
        local = mult(b, blk[level][...])
        bq = mult(b, bas[level][:, :RANK])
        lv = mult(local, bas[level][:, RANK:]) if level < 3 else None
        return local, bq, lv

    parts_of = [min(size[level], 16) for level in range(3)]

    def scatter_cross(level):
        g = size[level]
        p = parts_of[level]
        rp = RANK // p
        idx = me % g
        base = me - idx
        sem = sem_of(("rs", level))
        cross_p, rs_buf = m["cross_p", level], m["rs", level]

        def body(k, carry):
            q = (idx + k) % p

            def go():
                rows = pl.ds(pl.multiple_of(q * rp, 8), rp)
                remote(cross_p.at[rows], rs_buf.at[idx], sem, base + q).start()

            if g == p:
                go()
            else:
                pl.when(q != idx)(go)
            return carry

        lax.fori_loop(1 if g == p else 0, p, body, 0)

        def keep():
            rows = pl.ds(pl.multiple_of(idx * rp, 8), rp)
            rs_buf[idx] = cross_p[rows, :]

        if g == p:
            keep()
        else:
            pl.when(idx < p)(keep)

    def ship_couple(level):
        gp = size[level + 1]
        u = ups[level]
        cap = caps[level]
        wide = max(8, cap)
        sep = gp * LANES
        t = tgt[level][...]
        upd = t >= sep
        rel = jnp.where(upd, t - sep, t)
        dst = rel // LANES
        low = rel % LANES + jnp.where(upd, LANES, 0)
        ri = lax.broadcasted_iota(jnp.int32, (u, u), 0)
        ci = lax.broadcasted_iota(jnp.int32, (u, u), 1)
        dst_f = dst.astype(F32)
        dst_c = jnp.sum(jnp.where(ri == ci, jnp.broadcast_to(dst_f, (u, u)), 0.0), axis=1, keepdims=True)
        rank = jnp.sum(
            jnp.where((dst_c == dst_f) & (ri < ci), 1.0, 0.0), axis=0, keepdims=True
        ).astype(jnp.int32)
        pos = dst * wide + rank
        slots = gp * wide
        si = lax.broadcasted_iota(jnp.int32, (slots, u), 0)
        hit = (si == pos).astype(F32)
        moved = mult(hit, cpl[level][...])
        perm_buf, recv_c = m["perm", level], m["couple", level]
        if cap <= 4:
            shifted = (si == pos + 4).astype(F32)
            lowc = jnp.sum(shifted * low.astype(F32), axis=1, keepdims=True)
            both = moved + jnp.broadcast_to(lowc, (slots, LANES))
        else:
            lowc = jnp.sum(hit * low.astype(F32), axis=1, keepdims=True)
            both = jnp.concatenate([moved, jnp.broadcast_to(lowc, (slots, LANES))], axis=1)
        perm_buf[...] = both.reshape(gp, wide, both.shape[1])
        idx = me % gp
        recv_c[idx] = perm_buf[idx]
        send_each(lambda q: perm_buf.at[q], lambda i: recv_c.at[i], gp, ("couple", level))
        pending.append((perm_buf.at[pl.ds(0, gp - 1)], sem_of(("couple", level))))

    def gather_cross(level):
        g = size[level]
        gp = size[level + 1]
        p = parts_of[level]
        idx = me % g
        place = me % gp
        sem = sem_of(("cross", level))
        slot = place // g * p + idx
        buf, rs_buf = m["cross", level], m["rs", level]

        def go():
            wait_for(rs_buf.at[pl.ds(0, g - 1)], recv_sem.at[sem_of(("rs", level))])
            buf[slot] = jnp.sum(rs_buf[...], axis=0)

            def body(k, carry):
                peer = me - place + (place + k) % gp
                remote(buf.at[slot], buf.at[slot], sem, peer).start()
                return carry

            lax.fori_loop(1, gp, body, 0)

        if g == p:
            go()
        else:
            pl.when(idx < p)(go)

    def build_gt(level):
        g = size[level]
        gp = size[level + 1]
        wide = max(8, caps[level])
        nch = gp // g
        gt = m["gt", level]
        rows = gt.shape[1]
        arrive(("couple", level), gp)
        slots = g * wide
        lane = lax.broadcasted_iota(jnp.int32, (slots, rows), 1).astype(F32)
        for child in range(nch):
            got = m["couple", level][child * g : (child + 1) * g]
            got = got.reshape(slots, got.shape[2])
            if caps[level] <= 4:
                up = jnp.concatenate([got[4:, :1], got[:4, :1]], axis=0)
                si = lax.broadcasted_iota(jnp.int32, (slots, 1), 0)
                low = jnp.where(si % 8 < 4, up, -1.0)
            else:
                low = got[:, LANES : LANES + 1]
            ot = (lane == low).astype(F32)
            gt[child * RANK : (child + 1) * RANK, :] = inner(got[:, :LANES], ot)

    def arrive_cross(level):
        g = size[level]
        p = parts_of[level]
        n = size[level + 1] // g * p
        sem = recv_sem.at[sem_of(("cross", level))]
        buf = m["cross", level]
        if g == p:
            wait_for(buf.at[pl.ds(0, n - 1)], sem)
        else:
            idx = me % g
            pl.when(idx < p)(lambda: wait_for(buf.at[pl.ds(0, n - 1)], sem))
            pl.when(idx >= p)(lambda: wait_for(buf.at[pl.ds(0, n)], sem))

    def cross_of(level, child):
        p = parts_of[level]
        return m["cross", level][pl.ds(child * p, p)].reshape(RANK, RANK)

    def build_bot_middle():
        gp = size[2]
        place = me % gp
        rows = 2 * LANES
        ri = lax.broadcasted_iota(jnp.int32, (rows, LANES), 0)
        arrive("tgt_middle", gp)
        mine = jnp.where(ri < LANES, place * LANES + ri, (gp + place - 1) * LANES + ri).astype(F32)

        def fill(j, carry):
            t = m["tgt_middle"][j][0:1, :]
            lanes = pl.ds(pl.multiple_of(j * LANES, LANES), LANES)
            m["bot_middle"][:, lanes] = (mine == t).astype(F32).astype(BF16)
            return carry

        lax.fori_loop(0, gp, fill, 0)

    def build_bot_upper():
        rows = planes * LANES
        ri = lax.broadcasted_iota(jnp.int32, (rows, LANES), 0)
        arrive("tgt_upper", plane)
        mine = ((ri // LANES * plane + spot) * LANES + ri % LANES).astype(F32)

        def fill(j, carry):
            t = m["tgt_upper"][j][0:1, :]
            lanes = pl.ds(pl.multiple_of(j * LANES, LANES), LANES)
            m["bot_upper"][:, lanes] = (mine == t).astype(F32).astype(BF16)
            return carry

        lax.fori_loop(0, plane, fill, 0)

    def build_ft_middle():
        t = tgt[1][...]
        ri = lax.broadcasted_iota(jnp.int32, (LANES, LANES), 0)

        def fill(j, carry):
            rows = pl.ds(pl.multiple_of(j * LANES, LANES), LANES)
            m["ft_middle"][rows, :] = (ri + j * LANES == t).astype(F32).astype(BF16)
            return carry

        lax.fori_loop(0, m["ft_middle"].shape[0] // LANES, fill, 0)

    def build_ft_upper():
        arrive("tgt_layer", planes)
        t = jnp.concatenate([m["tgt_layer"][j][0:1, :] for j in range(planes)], axis=1)
        ri = lax.broadcasted_iota(jnp.int32, (LANES, planes * LANES), 0)

        def fill(j, carry):
            rows = pl.ds(pl.multiple_of(j * LANES, LANES), LANES)
            here = ((ri + (layer * plane + j) * LANES).astype(F32) == t).astype(F32)
            m["ft_upper"][rows, :] = here.astype(BF16)
            return carry

        lax.fori_loop(0, plane, fill, 0)

    def total_sum(value, name):
        m[name, "a"][spot] = value
        send_all((name, "a"), plane)
        arrive((name, "a"), plane)
        m[name, "b"][layer] = jnp.sum(m[name, "a"][...], axis=0)
        send_all((name, "b"), planes, plane)

    def total_arrived(name):
        arrive((name, "b"), planes)
        return jnp.sum(m[name, "b"][...], axis=0)

    def share(level, zp):
        m["zp", level][me % size[level]] = zp
        send_all(("zp", level), size[level])

    def shared(level):
        arrive(("zp", level), size[level])
        return jnp.sum(m["zp", level][...], axis=0)

    local, bq, lv = local_forward(0, src[0][...])
    m["f1"][spot] = jnp.concatenate([bq, lv], axis=0)
    m["cross_p", 0][...] = inner(exp[0][...], bas[0][:, RANK:])
    pl.semaphore_wait(barrier, total_devices - 1)
    send_all("f1", plane)
    scatter_cross(0)
    ship_couple(0)
    for level in (1, 2):
        m["cross_p", level][...] = inner(exp[level][...], bas[level][:, RANK:])
        scatter_cross(level)
    m["tgt_middle"][me % size[2]] = jnp.broadcast_to(tgt[1][...], (8, LANES)).astype(F32)
    send_all("tgt_middle", size[2])
    gather_cross(0)
    ship_couple(1)
    gather_cross(1)
    mine_t = jnp.broadcast_to(tgt[2][...], (8, LANES)).astype(F32)
    m["tgt_upper"][spot] = mine_t
    send_all("tgt_upper", plane)
    m["tgt_layer"][layer] = mine_t
    send_all("tgt_layer", planes, plane)
    build_gt(0)

    saved = []
    inc_upd = None
    for level in range(3):
        g = size[level]
        gp = size[level + 1]
        nch = gp // g
        place = me % gp
        parent = me // gp
        child_me = place // g
        arrive_cross(level)
        if level < 2:
            name = ("f1", "f2")[level]
            buf, step = m[name], g
            arrive(name, gp)
        else:
            buf, step = m["f3b"], g // plane
            arrive("f3b", planes)
        ws = []
        for child in range(nch):
            tot = jnp.sum(buf[child * step : (child + 1) * step, : 2 * count, :], axis=0)
            front = parent * nch + child
            hq = tot[:count] * mask(level, front, 0)
            cross = cross_of(level, child)
            ws.append((tot[count:] + mult(hq, cross)) * mask(level, front, 1))
        inc = -mult(jnp.concatenate(ws, axis=1), m["gt", level][...])
        if level == 1:
            rows = jnp.concatenate([buf[j, 2 * count : 3 * count, :] for j in range(gp)], axis=1)
            inc = inc + select(rows, m["bot_middle"][...], 1)
        if level == 2:
            inc = inc + jnp.sum(buf[:, 2 * count : 3 * count, :], axis=0)
        bn = src[level + 1][...] + inc[:, :LANES]
        local_n, bq_n, lv_n = local_forward(level + 1, bn)
        if level == 0:
            m["f2"][me % size[2]] = jnp.concatenate([bq_n, lv_n, inc[:, LANES:]], axis=0)
            send_all("f2", size[2])
        elif level == 1:
            m["f3a"][spot] = jnp.concatenate([bq_n, lv_n, inc[:, LANES:]], axis=0)
            send_all("f3a", plane)
        else:
            m["f4", "a"][spot] = bq_n
            send_all(("f4", "a"), plane)
        own = jnp.sum(buf[pl.ds(child_me * step, step), :count, :], axis=0)
        hq = own * mask(level, me // g, 0)
        z = (local + outer(hq, exp[level][...])) * piv[level][...]
        saved.append(z)
        share(level, mult(z, exp[level][...]))
        if level == 0:
            ship_couple(2)
            gather_cross(2)
            build_gt(1)
            build_bot_middle()
        elif level == 1:
            build_bot_upper()
            arrive("f3a", plane)
            sums = jnp.sum(m["f3a"][:, : 2 * count, :], axis=0)
            rows = jnp.concatenate([m["f3a"][j, 2 * count :, :] for j in range(plane)], axis=1)
            part = select(rows, m["bot_upper"][...], 1)
            for q in range(planes):
                m["f3s"][q] = jnp.concatenate([sums, part[:, q * LANES : (q + 1) * LANES]], axis=0)
            m["f3b"][layer] = m["f3s"][layer]
            send_each(lambda q: m["f3s"].at[q], lambda i: m["f3b"].at[i], planes, "f3b", plane)
            pending.append((m["f3s"].at[pl.ds(0, planes - 1)], sem_of("f3b")))
            build_gt(2)
        else:
            arrive(("f4", "a"), plane)
            m["f4", "b"][layer] = jnp.sum(m["f4", "a"][...], axis=0)
            send_all(("f4", "b"), planes, plane)
        local = local_n

    build_ft_upper()
    hq = total_arrived("f4") * mask(3, 0, 0)
    z = (local + outer(hq, exp[3][...])) * piv[3][...]
    total_sum(mult(z, exp[3][...]), "f5")
    if not late:
        build_ft_middle()
    x = outer(z, blk[3][...])
    rp_total = total_arrived("f5") * mask(3, 0, 0)
    x = x + outer(rp_total, bas[3][:, :RANK])

    xu = None
    for level in (2, 1, 0):
        g = size[level]
        gp = size[level + 1]
        nch = gp // g
        place = me % gp
        child_me = place // g
        full = x if xu is None else jnp.concatenate([x, xu], axis=1)
        sp = outer(full, m["gt", level][...])
        pieces = [sp[:, c * RANK : (c + 1) * RANK] for c in range(nch)]
        if level == 2:
            m["b1a"][spot] = jnp.concatenate(pieces + [x], axis=0)
            send_all("b1a", plane)
            outs[3][...] = x
            arrive("b1a", plane)
            o = nch * count
            sums = jnp.sum(m["b1a"][:, :o, :], axis=0)
            rows = jnp.concatenate([m["b1a"][j, o:, :] for j in range(plane)], axis=1)
            part = select(rows, m["ft_upper"][...], 0)
            for q in range(planes):
                c = q * plane // g
                m["b1s"][q] = jnp.concatenate(
                    [sums[c * count : (c + 1) * count], part[:, q * LANES : (q + 1) * LANES]], axis=0
                )
            m["b1b"][layer] = m["b1s"][layer]
            send_each(lambda q: m["b1s"].at[q], lambda i: m["b1b"].at[i], planes, "b1b", plane)
            pending.append((m["b1s"].at[pl.ds(0, planes - 1)], sem_of("b1b")))
            arrive("b1b", planes)
            both = jnp.sum(m["b1b"][...], axis=0)
            s, xu = both[:count], both[count:]
        else:
            name = ("b3", "b2")[level]
            buf, piece = m[name], m["piece", level]
            for c in range(nch):
                piece[c] = pieces[c]
            head = pl.ds(0, count)
            rest = pl.ds(count, 2 * count)
            buf[place, head] = piece[child_me]
            if level == 1:
                buf[place, rest] = jnp.concatenate([x, xu], axis=0)

                def ship(k, carry, gp=gp, g=g, place=place, buf=buf, piece=piece, name=name):
                    q = (place + k) % gp
                    peer = me - place + q
                    sem = sem_of(name)
                    remote(piece.at[q // g], buf.at[place, head], sem, peer).start()
                    remote(buf.at[place, rest], buf.at[place, rest], sem, peer).start()
                    return carry

                lax.fori_loop(1, gp, ship, 0)
            else:
                send_each(lambda q: piece.at[q // g], lambda i: buf.at[i], gp, name)
            pending.append((buf.at[pl.ds(0, gp - 1)], sem_of(name)))
            outs[level + 1][...] = x
            arrive(name, gp)
            s = jnp.sum(buf[:, head, :], axis=0)
            if level == 1:
                blocks = [buf[j, count : 2 * count, :] for j in range(gp)]
                blocks += [buf[j, 2 * count :, :] for j in range(gp)]
                if late:
                    build_ft_middle()
                xu = select(jnp.concatenate(blocks, axis=1), m["ft_middle"][...], 0)
        s = s * mask(level, me // g, 1)
        r = saved[level] - outer(s, bas[level][:, RANK:])
        proj = (shared(level) - outer(s, cross_of(level, child_me))) * mask(level, me // g, 0)
        x = outer(r, blk[level][...]) + outer(proj, bas[level][:, :RANK])
    outs[0][...] = x

    for part, sem in pending:
        wait_for(part, send_sem.at[sem])
    for level in range(3):
        g = size[level]
        p = parts_of[level]
        rp = RANK // p
        n = size[level + 1] // g * p
        idx = me % g
        rs_sem = send_sem.at[sem_of(("rs", level))]
        ag_sem = send_sem.at[sem_of(("cross", level))]
        cross_p, buf = m["cross_p", level], m["cross", level]

        def ag_done():
            for _ in range(g // p - 1):
                wait_for(buf.at[pl.ds(0, n)], ag_sem)
            wait_for(buf.at[pl.ds(0, n - 1)], ag_sem)

        if g == p:
            wait_for(cross_p.at[pl.ds(0, (p - 1) * rp)], rs_sem)
            ag_done()
        else:
            pl.when(idx < p)(lambda: wait_for(cross_p.at[pl.ds(0, (p - 1) * rp)], rs_sem))
            pl.when(idx >= p)(lambda: wait_for(cross_p, rs_sem))
            pl.when(idx < p)(ag_done)


def solution(mesh):
    leaves, across = mesh.shape["leaf"], mesh.shape["grid"]

    def shards(*args):
        levels = [args[8 * i : 8 * i + 8] for i in range(3)]
        root = args[24:30]
        (sl, bl, el, qs, pv, cl, rk, tg) = zip(*levels)
        src = list(sl) + [root[0]]
        blk = list(bl) + [root[1]]
        exp = list(el) + [root[2]]
        bas = list(qs) + [root[3]]
        piv = [v.reshape(1, -1) for v in list(pv) + [root[4]]]
        rnk = list(rk) + [root[5]]
        tgt = [t.reshape(1, -1) for t in tg]
        count = src[0].shape[0]
        ups = [t.shape[1] for t in tgt]
        fronts = [r.shape[0] for r in rnk]
        size = [leaves * across // f for f in fronts]
        for v in src:
            assert v.shape[1] == LANES
        vm = lambda *s: pltpu.VMEM(s, F32)
        bits = lambda *s: pltpu.VMEM(s, BF16)
        total = leaves * across
        plane = size[1]
        planes = total // plane
        nch = [size[i + 1] // size[i] for i in range(3)]
        caps = [max(1, -(-ups[i] // size[i + 1])) for i in range(3)]
        parts = [min(size[i], 16) for i in range(3)]
        ft = (size[2] * 2 * LANES, LANES)
        bufs = {
            "f1": vm(plane, 2 * count, LANES),
            "f2": vm(size[2], 3 * count, LANES),
            "f3a": vm(plane, 3 * count, LANES),
            "f3s": vm(planes, 3 * count, LANES),
            "f3b": vm(planes, 3 * count, LANES),
            "b1a": vm(plane, (nch[2] + 1) * count, LANES),
            "b1s": vm(planes, 2 * count, LANES),
            "b1b": vm(planes, 2 * count, LANES),
            "b2": vm(size[2], 3 * count, LANES),
            "b3": vm(size[1], count, LANES),
            "tgt_middle": vm(size[2], 8, LANES),
            "tgt_upper": vm(plane, 8, LANES),
            "tgt_layer": vm(planes, 8, LANES),
            "bot_middle": bits(2 * LANES, size[2] * LANES),
            "bot_upper": bits(planes * LANES, plane * LANES),
            "ft_middle": bits(*ft),
            "ft_upper": bits(plane * LANES, planes * LANES),
        }
        for name in ("f4", "f5"):
            bufs[name, "a"] = vm(plane, count, LANES)
            bufs[name, "b"] = vm(planes, count, LANES)
        for i in range(3):
            wide = LANES if caps[i] <= 4 else 2 * LANES
            bufs["perm", i] = vm(size[i + 1], max(8, caps[i]), wide)
            bufs["couple", i] = vm(size[i + 1], max(8, caps[i]), wide)
            bufs["cross_p", i] = vm(RANK, RANK)
            bufs["rs", i] = vm(size[i], RANK // parts[i], RANK)
            bufs["cross", i] = vm(nch[i] * parts[i], RANK // parts[i], RANK)
            bufs["gt", i] = vm(nch[i] * RANK, LANES * (1 if i == 2 else 2))
            bufs["zp", i] = vm(size[i], count, LANES)
            bufs["piece", i] = vm(nch[i], count, LANES)
        scratch = list(bufs.values())
        scratch += [pltpu.SemaphoreType.DMA((40,)), pltpu.SemaphoreType.DMA((40,))]
        vspec = pl.BlockSpec(memory_space=pltpu.VMEM)
        sspec = pl.BlockSpec(memory_space=pltpu.SMEM)
        return pl.pallas_call(
            functools.partial(kernel, (leaves, across, size, ups, count, caps), list(bufs)),
            out_shape=[jax.ShapeDtypeStruct(v.shape, F32) for v in src],
            in_specs=[vspec] * 20 + [sspec] * 4 + [vspec] * 6,
            out_specs=[vspec] * 4,
            scratch_shapes=scratch,
            compiler_params=pltpu.CompilerParams(
                collective_id=0, has_side_effects=True, vmem_limit_bytes=60 * 1024 * 1024
            ),
        )(*src, *blk, *exp, *bas, *piv, *rnk, *cl, *tgt)

    spread = ("leaf", "grid")
    level = (P(None, spread), P(spread, None), P(spread, None), P(spread, None), P(spread))
    mid = level + (P(spread, None), P(), P(spread))
    return jax.shard_map(
        shards,
        mesh=mesh,
        in_specs=mid * 3 + level + (P(),),
        out_specs=(P(None, spread),) * 4,
        check_vma=False,
    )
```

time: 92.3 us -> 76.7 us (0.83)
  Pallas kernels: 86.1 us -> 70.4 us
    pallas_call x1, Pallas kernels: 86.1 us -> 70.4 us  [shards(): pl.pallas_call(functools.partial(kernel, (leaves, across, size, ups, coun...]
where the time goes in v2:
time: 76.7 us; the launch traced here: 76.4 us
  Pallas kernels  70.4 us (92%)
  local copies, waits for them, and re-layouts  5.31 us (7%)
    pallas_call x1, Pallas kernels, shards(): pl.pallas_call(functools.partial(kernel, (leaves, across, size, ups, coun...  70.4 us
    unnamed x18, local copies, waits for them, and re-layouts  5.31 us

profile of v2, /device:TPU:0, one launch (start us, length us, event | category | flops | bytes accessed | tf_op | source)
XLA Modules:
  0.0 76.4 jit_solution(6843461874204579568)
XLA Ops:
  0.6 0.0 copy-start.4
  0.6 0.7 copy-done.4
  1.3 0.0 copy-start.5
  1.3 0.7 copy.35.refs_21_
  2.0 0.0 copy-done.5
  2.0 0.7 copy.34.refs_20_
  2.7 70.4 %shard_map.309 = (f32[8,128]{1,0:T(8,128)}, f32[8,128]{1,0:T(8,128)}, f32[8,128]{1,0:T(8,128)}, f32[8,128]{1,0:T(8,128)}) custom-call(f32[8,128]{1,0:T(8,128)} %refs_0_.1, f32[8,128]{1,0:T(8,128)} %refs_1_.1, f32[8,128]{1,0:T(8,128)} %refs_2_.1, f32[8,128]{1,0:T(8,128)} %refs_3_.1, f32[128,128]{1,0:T(8,128)} %refs_4_.1, f32[128,128]{1,0:T(8,128)} %refs_5_.1, ...), custom_call_target="tpu_custom_call" | custom-call | tf_op jit(solution)/shard_map/pallas_call | solution.py:599
  73.1 0.0 copy-start.3
  73.1 0.7 copy-done.3
  73.8 0.0 copy-start.2
  73.8 0.6 copy.40
  74.4 0.1 copy-done.2
  74.5 0.0 copy-start.1
  74.5 0.6 copy.41
  75.1 0.1 copy-done.1
  75.2 0.0 copy-start
  75.2 0.6 copy.42
  75.7 0.1 copy-done
  75.8 0.6 copy.43
Async XLA Ops:
  0.6 0.7 copy-start.4
  1.3 0.7 copy-start.5
  73.1 0.7 copy-start.3
  73.8 0.7 copy-start.2
  74.5 0.7 copy-start.1
  75.2 0.7 copy-start

commit v3 on v2

--- a/solution.py
+++ b/solution.py
@@ -10,15 +10,34 @@
 RANK = 128
 LANES = 128
 MESH = pl.DeviceIdType.MESH
-HIGHEST = lax.Precision.HIGHEST
 F32 = jnp.float32
 BF16 = jnp.bfloat16
 
 
-def dot(a, b, ca, cb, precision=HIGHEST):
-    return lax.dot_general(
-        a, b, (((ca,), (cb,)), ((), ())), precision=precision, preferred_element_type=F32
-    )
+def once(a, b, ca, cb):
+    return lax.dot_general(a, b, (((ca,), (cb,)), ((), ())), preferred_element_type=F32)
+
+
+def halves(x):
+    hi = x.astype(BF16)
+    return hi, (x - hi.astype(F32)).astype(BF16)
+
+
+def dot(a, b, ca, cb):
+    ah, al = halves(a)
+    bh, bl = halves(b)
+    if ca == 0:
+        return once(ah, bh, ca, cb) + (once(al, bh, ca, cb) + once(ah, bl, ca, cb))
+    n = a.shape[0]
+    both = once(jnp.concatenate([ah.astype(F32), al.astype(F32)], axis=0).astype(BF16), bh, ca, cb)
+    return both[:n] + (both[n:] + once(ah, bl, ca, cb))
+
+
+def pieces3(x):
+    hi = x.astype(BF16)
+    rest = x - hi.astype(F32)
+    mid = rest.astype(BF16)
+    return hi, mid, (rest - mid.astype(F32)).astype(BF16)
 
 
 def mult(a, b):
@@ -41,7 +60,7 @@
 
 
 def select(x, onehot, cb):
-    out = dot(split3(x), onehot, 1, cb, lax.Precision.DEFAULT)
+    out = once(split3(x), onehot, 1, cb)
     n = x.shape[0]
     return out[:n] + out[n : 2 * n] + out[2 * n :]
 
@@ -183,7 +202,9 @@
         slots = gp * wide
         si = lax.broadcasted_iota(jnp.int32, (slots, u), 0)
         hit = (si == pos).astype(F32)
-        moved = mult(hit, cpl[level][...])
+        hit16 = hit.astype(BF16)
+        hi, mid, lo = [once(hit16, piece, 1, 0) for piece in pieces3(cpl[level][...])]
+        moved = hi + mid + lo
         perm_buf, recv_c = m["perm", level], m["couple", level]
         if cap <= 4:
             shifted = (si == pos + 4).astype(F32)
@@ -243,8 +264,9 @@
                 low = jnp.where(si % 8 < 4, up, -1.0)
             else:
                 low = got[:, LANES : LANES + 1]
-            ot = (lane == low).astype(F32)
-            gt[child * RANK : (child + 1) * RANK, :] = inner(got[:, :LANES], ot)
+            ot = (lane == low).astype(F32).astype(BF16)
+            hi, mid, lo = [once(piece, ot, 0, 0) for piece in pieces3(got[:, :LANES])]
+            gt[child * RANK : (child + 1) * RANK, :] = hi + mid + lo
 
     def arrive_cross(level):
         g = size[level]

time: 76.7 us -> 72.7 us (0.948)
  Pallas kernels: 70.4 us -> 66.4 us
    pallas_call x1, Pallas kernels: 70.4 us -> 66.4 us  [shards(): pl.pallas_call(functools.partial(kernel, (leaves, across, size, ups, coun...]
where the time goes in v3:
time: 72.7 us; the launch traced here: 72.4 us
  Pallas kernels  66.4 us (91%)
  local copies, waits for them, and re-layouts  5.31 us (7%)
    pallas_call x1, Pallas kernels, shards(): pl.pallas_call(functools.partial(kernel, (leaves, across, size, ups, coun...  66.4 us
    unnamed x18, local copies, waits for them, and re-layouts  5.31 us

profile of v3, /device:TPU:0, one launch (start us, length us, event | category | flops | bytes accessed | tf_op | source)
XLA Modules:
  0.0 72.4 jit_solution(1159341484944557312)
XLA Ops:
  0.6 0.0 copy-start.4
  0.6 0.7 copy-done.4
  1.3 0.0 copy-start.5
  1.3 0.7 copy.35.refs_21_
  2.0 0.0 copy-done.5
  2.0 0.7 copy.34.refs_20_
  2.7 66.4 %shard_map.309 = (f32[8,128]{1,0:T(8,128)}, f32[8,128]{1,0:T(8,128)}, f32[8,128]{1,0:T(8,128)}, f32[8,128]{1,0:T(8,128)}) custom-call(f32[8,128]{1,0:T(8,128)} %refs_0_.1, f32[8,128]{1,0:T(8,128)} %refs_1_.1, f32[8,128]{1,0:T(8,128)} %refs_2_.1, f32[8,128]{1,0:T(8,128)} %refs_3_.1, f32[128,128]{1,0:T(8,128)} %refs_4_.1, f32[128,128]{1,0:T(8,128)} %refs_5_.1, ...), custom_call_target="tpu_custom_call" | custom-call | tf_op jit(solution)/shard_map/pallas_call | solution.py:621
  69.1 0.0 copy-start.3
  69.1 0.7 copy-done.3
  69.8 0.0 copy-start.2
  69.8 0.6 copy.40
  70.4 0.1 copy-done.2
  70.4 0.0 copy-start.1
  70.4 0.6 copy.41
  71.0 0.1 copy-done.1
  71.1 0.0 copy-start
  71.1 0.6 copy.42
  71.7 0.1 copy-done
  71.8 0.6 copy.43
Async XLA Ops:
  0.6 0.7 copy-start.4
  1.3 0.7 copy-start.5
  69.1 0.7 copy-start.3
  69.8 0.7 copy-start.2
  70.4 0.7 copy-start.1
  71.1 0.7 copy-start

commit v4 on v3

--- a/solution.py
+++ b/solution.py
@@ -180,7 +180,7 @@
         else:
             pl.when(idx < p)(keep)
 
-    def ship_couple(level):
+    def pack_couple(level):
         gp = size[level + 1]
         u = ups[level]
         cap = caps[level]
@@ -216,6 +216,10 @@
         perm_buf[...] = both.reshape(gp, wide, both.shape[1])
         idx = me % gp
         recv_c[idx] = perm_buf[idx]
+
+    def ship_couple(level):
+        gp = size[level + 1]
+        perm_buf, recv_c = m["perm", level], m["couple", level]
         send_each(lambda q: perm_buf.at[q], lambda i: recv_c.at[i], gp, ("couple", level))
         pending.append((perm_buf.at[pl.ds(0, gp - 1)], sem_of(("couple", level))))
 
@@ -360,13 +364,14 @@
 
     local, bq, lv = local_forward(0, src[0][...])
     m["f1"][spot] = jnp.concatenate([bq, lv], axis=0)
-    m["cross_p", 0][...] = inner(exp[0][...], bas[0][:, RANK:])
+    for level in range(3):
+        m["cross_p", level][...] = inner(exp[level][...], bas[level][:, RANK:])
+        pack_couple(level)
     pl.semaphore_wait(barrier, total_devices - 1)
     send_all("f1", plane)
     scatter_cross(0)
     ship_couple(0)
     for level in (1, 2):
-        m["cross_p", level][...] = inner(exp[level][...], bas[level][:, RANK:])
         scatter_cross(level)
     m["tgt_middle"][me % size[2]] = jnp.broadcast_to(tgt[1][...], (8, LANES)).astype(F32)
     send_all("tgt_middle", size[2])

time: 72.7 us -> 72.8 us (level)
  no operation moved by 1% of the time
where the time goes in v4:
time: 72.8 us; the launch traced here: 72.5 us
  Pallas kernels  66.6 us (91%)
  local copies, waits for them, and re-layouts  5.31 us (7%)
    pallas_call x1, Pallas kernels, shards(): pl.pallas_call(functools.partial(kernel, (leaves, across, size, ups, coun...  66.6 us
    unnamed x18, local copies, waits for them, and re-layouts  5.31 us

profile of v4, /device:TPU:0, one launch (start us, length us, event | category | flops | bytes accessed | tf_op | source)
XLA Modules:
  0.0 72.5 jit_solution(9325366277446140820)
XLA Ops:
  0.6 0.0 copy-start.4
  0.6 0.7 copy-done.4
  1.3 0.0 copy-start.5
  1.3 0.7 copy.35.refs_21_
  2.0 0.0 copy-done.5
  2.0 0.7 copy.34.refs_20_
  2.7 66.6 %shard_map.309 = (f32[8,128]{1,0:T(8,128)}, f32[8,128]{1,0:T(8,128)}, f32[8,128]{1,0:T(8,128)}, f32[8,128]{1,0:T(8,128)}) custom-call(f32[8,128]{1,0:T(8,128)} %refs_0_.1, f32[8,128]{1,0:T(8,128)} %refs_1_.1, f32[8,128]{1,0:T(8,128)} %refs_2_.1, f32[8,128]{1,0:T(8,128)} %refs_3_.1, f32[128,128]{1,0:T(8,128)} %refs_4_.1, f32[128,128]{1,0:T(8,128)} %refs_5_.1, ...), custom_call_target="tpu_custom_call" | custom-call | tf_op jit(solution)/shard_map/pallas_call | solution.py:626
  69.2 0.0 copy-start.3
  69.2 0.7 copy-done.3
  69.9 0.0 copy-start.2
  69.9 0.6 copy.40
  70.5 0.1 copy-done.2
  70.6 0.0 copy-start.1
  70.6 0.6 copy.41
  71.2 0.1 copy-done.1
  71.3 0.0 copy-start
  71.3 0.6 copy.42
  71.9 0.1 copy-done
  71.9 0.6 copy.43
Async XLA Ops:
  0.6 0.7 copy-start.4
  1.3 0.7 copy-start.5
  69.2 0.7 copy-start.3
  69.9 0.7 copy-start.2
  70.6 0.7 copy-start.1
  71.3 0.7 copy-start
